TPU v7x, 32 devices: a whole 2x2x4 slice. The times are simulated.
32 devices in a mesh: row: 4 (over y, x), col: 4 (over z), rep: 2 (over core).
Axes of the slice: x: 2, y: 2, z: 4, core: 2. Of those that a mesh axis runs over, the one named last changes fastest.
Arguments:
- sources: int32 [64], replicated, may hold values from 0 to 4095
- tile_weights: int32 [1024, 128, 128], P(('row', 'col', 'rep')), may hold values from 0 to 16, as said below
- tile_src: int32 [1024], P(('row', 'col', 'rep')), may hold values from 0 to 31, as said below
- tile_dst: int32 [1024], P(('row', 'col', 'rep')), may hold values from 0 to 31, as said below
- tile_count: int32 [32], P(('row', 'col', 'rep')), may hold values from 1 to 32, 512 in all
Outputs:
- distances: float32 [64, 4096], P(None, ('row', 'col', 'rep'))
- recip_sums: float32 [16, 64], P(('row', 'col'))
Inputs may be any that keep to these rules, and one draw needn't show every extreme that they name: `tile_weights`: an entry of 0 means no edge; others are the edge's weight. `tile_src`: piece p = b // 1 of block b belongs to the device at mesh coordinates (row, col, rep) = (p // 8, (p // 2) % 4, p % 2); slot k belongs to device k // 32 in the same numbering. A tile's source block lies in a piece whose col index is that of the tile's device. `tile_dst`: A tile's destination block lies in a piece whose row and rep indices are those of the tile's device, in the numbering given for tile_src. Only the first tile_count[d] slots of device d hold live tiles; some device has all 32 slots live.
All inputs are finite; a program needn't handle non-finite values.
Results may differ from a plain program's by a relative error of at most 0.0003.
Values may be sent and summed in bfloat16 or wider, within the bound.
No kernel may reach another device: no remote copies, remote signals or barrier semaphores. Data moves between devices by JAX's collectives and lax.ppermute only.
A program may use at most 64 MiB of HBM per device.

v0:
```python
import jax
import jax.numpy as jnp
from jax import lax
from jax.sharding import PartitionSpec as P

BLK_DEV = 1
TILE_DEV = 32
BS = 128
ROUNDS = 2


far_value = 255.0


def relax_tiles(gathered, weights, src_pos, dst_pos, ordering, live_total, blocks_out):
    height = gathered.shape[0]
    partial_value = jnp.full((height, blocks_out * BS), far_value, jnp.bfloat16)

    def relax_four(step_no, partial_value):
        for offset in range(4):
            slot_now = 4 * step_no + offset
            picked = ordering[slot_now]
            weight = lax.dynamic_index_in_dim(weights, picked, 0, keepdims=False)
            source = lax.dynamic_slice_in_dim(gathered, src_pos[picked] * BS, BS, 1)
            candidate = jnp.min(source[:, :, None] + weight[None, :, :], axis=1)
            candidate = jnp.where(slot_now < live_total, candidate, jnp.bfloat16(far_value))
            begin_at = dst_pos[picked] * BS
            previous = lax.dynamic_slice_in_dim(partial_value, begin_at, BS, 1)
            partial_value = lax.dynamic_update_slice_in_dim(
                partial_value, jnp.minimum(previous, candidate), begin_at, 1
            )
        return partial_value

    return lax.fori_loop(0, (live_total + 3) // 4, relax_four, partial_value)


def source_slot(block_ids, n_col, n_rep):
    piece_id = block_ids // BLK_DEV
    return (piece_id // (n_col * n_rep) * n_rep + piece_id % n_rep) * BLK_DEV + block_ids % BLK_DEV


def per_device(sources, tile_weights, tile_src, tile_dst, tile_count):
    n_col = lax.axis_size("col")
    n_rep = lax.axis_size("rep")
    width = BLK_DEV * BS
    sources_all = sources.shape[0]
    piece_id = (lax.axis_index("row") * n_col + lax.axis_index("col")) * n_rep + lax.axis_index(
        "rep"
    )
    columns = piece_id * width + jnp.arange(width, dtype=jnp.int32)
    dist = jnp.where(columns[None, :] == sources[:, None], 0.0, far_value).astype(jnp.bfloat16)
    weights = jnp.where(tile_weights > 0, tile_weights.astype(jnp.float32), far_value).astype(
        jnp.bfloat16
    )
    ordering = jnp.arange(TILE_DEV, dtype=jnp.int32)
    live_total = tile_count[0]
    src_pos = source_slot(tile_src, n_col, n_rep)
    dest_piece = tile_dst // BLK_DEV
    dst_pos = dest_piece // n_rep % n_col * BLK_DEV + tile_dst % BLK_DEV
    for round_no in range(ROUNDS):
        gathered = lax.all_gather(dist, ("row", "rep"), axis=1, tiled=True)
        partial_value = relax_tiles(
            gathered, weights, src_pos, dst_pos, ordering, live_total, n_col * BLK_DEV
        )
        fresh = jnp.min(
            lax.all_to_all(
                partial_value.reshape(sources_all, 1, n_col * width),
                "col",
                split_axis=2,
                concat_axis=1,
                tiled=True,
            ),
            axis=1,
        )
        dist = jnp.minimum(dist, fresh)
    as_float = dist.astype(jnp.float32)
    inverse = jnp.where(as_float > 0, 1.0 / jnp.maximum(as_float, 1.0), 0.0)
    sums = lax.psum(jnp.sum(inverse, axis=1), "rep")
    return (as_float, sums[None, :])


def solution(mesh):
    return jax.shard_map(
        per_device,
        mesh=mesh,
        in_specs=(
            P(),
            P(("row", "col", "rep"), None, None),
            P(("row", "col", "rep")),
            P(("row", "col", "rep")),
            P(("row", "col", "rep")),
        ),
        out_specs=(P(None, ("row", "col", "rep")), P(("row", "col"), None)),
        check_vma=False,
    )
```

profile of v0, /device:TPU:0, one launch (start us, length us, event | category | flops | bytes accessed | tf_op | source)
XLA Modules:
  0.0 408.1 jit_solution(2897030421059010277)
XLA Ops:
  1.3 0.7 select_convert_fusion.1
  2.1 10.5 %all_gather.6 = bf16[64,1024]{1,0:T(8,128)(2,1)S(1)} all-gather(bf16[64,128]{1,0:T(8,128)(2,1)S(1)} %select_convert_fusion.1), channel_id=1, replica_groups=mesh['row'=4,'col'=4,'rep'=2] {'row','rep'}, dimensions={1}, use_global_device_ids=true | all-gather | bytes 147456 | tf_op jit(solution)/shard_map/all_gather | solution.py:61
  12.6 2.6 select_convert_fusion
  15.3 44.6 %while.26 = (s32[]{:T(128)}, bf16[64,512]{1,0:T(8,128)(2,1)S(1)}, s32[]{:T(128)}, s32[32]{0:T(128)S(1)}, s32[32]{0:T(128)S(1)}, /*index=5*/s32[]{:T(128)}, s32[3...) while((s32[]{:T(128)}, bf16[64,512]{1,0:T(8,128)(2,1)S(1)}, ...), condition=%wide.region_5.6_spmd.clone, body=%wide.region_0.5_spmd.clone.sunk | while | flops 8519746 | bytes 853061 | solution.py:34
  23.6 0.7 fusion.14
  26.9 1.4 add_reduce_fusion.18
  28.2 1.4 add_reduce_fusion.17
  29.6 1.4 add_reduce_fusion.16
  34.9 1.4 add_reduce_fusion.19
  45.9 0.7 fusion.14
  49.2 1.4 add_reduce_fusion.18
  50.5 1.4 add_reduce_fusion.17
  51.9 1.4 add_reduce_fusion.16
  57.1 1.4 add_reduce_fusion.19
  60.6 1.4 reduce.4
  62.0 0.8 reshape.63
  62.8 138.6 %all-to-all-start = ((bf16[4,2,4096]{2,1,0:T(2,128)(2,1)}), bf16[4,2,4096]{2,1,0:T(2,128)(2,1)S(1)}, u32[]{:S(2)}, u32[]{:S(2)}) async-start(bf16[4,2,4096]{2,1,0:T(2,128)(2,1)} %reshape.63), calls=%async_computation | async-start | bytes 131072 | tf_op jit(solution)/shard_map/all_to_all | solution.py:66
  201.4 5.7 %all-to-all-done = bf16[4,2,4096]{2,1,0:T(2,128)(2,1)S(1)} async-done(((bf16[4,2,4096]{2,1,0:T(2,128)(2,1)}), bf16[4,2,4096]{2,1,0:T(2,128)(2,1)S(1)}, u32[]{:S(2)}, u32[]{:S(2)}) %all-to-all-start) | async-done | bytes 65568 | tf_op jit(solution)/shard_map/all_to_all | solution.py:66
  207.6 9.0 %all_gather.7 = bf16[64,1024]{1,0:T(8,128)(2,1)S(1)} all-gather(bf16[64,128]{1,0:T(8,128)(2,1)S(1)} %fusion), channel_id=1, replica_groups=mesh['row'=4,'col'=4,'rep'=2] {'row','rep'}, dimensions={1}, use_global_device_ids=true | all-gather | bytes 147456 | tf_op jit(solution)/shard_map/all_gather | solution.py:61
  216.7 44.5 %while.27 = (s32[]{:T(128)}, bf16[64,512]{1,0:T(8,128)(2,1)S(1)}, s32[]{:T(128)}, s32[32]{0:T(128)S(1)}, s32[32]{0:T(128)S(1)}, /*index=5*/s32[]{:T(128)}, s32[3...) while((s32[]{:T(128)}, bf16[64,512]{1,0:T(8,128)(2,1)S(1)}, ...), condition=%wide.region_12.13_spmd.clone, body=%wide.region_7.12_spmd.clone.sunk | while | flops 8519746 | bytes 853061 | solution.py:34
  228.2 1.4 add_reduce_fusion.22
  229.6 1.4 add_reduce_fusion.21
  230.9 1.4 add_reduce_fusion.20
  236.2 1.4 add_reduce_fusion.23
  250.4 1.4 add_reduce_fusion.22
  251.8 1.4 add_reduce_fusion.21
  253.2 1.4 add_reduce_fusion.20
  258.4 1.4 add_reduce_fusion.23
  261.3 1.4 reduce.5
  262.9 141.0 %all_to_all.24 = bf16[4,2,4096]{2,1,0:T(2,128)(2,1)S(1)} all-to-all(bf16[4,2,4096]{2,1,0:T(2,128)(2,1)S(1)} %reshape.65), channel_id=1, replica_groups=mesh['row'=4,'col'=4,'rep'=2] {'col'}, dimensions={0} | all-to-all | bytes 131072 | tf_op jit(solution)/shard_map/all_to_all | solution.py:66
  404.3 0.8 select_reduce_fusion
  405.1 3.0 psum.7
  (55 shorter events, 6.6 us)
Async XLA Ops:
  0.6 14.6 %copy-start.2 = (s32[32]{0:T(128)S(1)}, s32[32]{0:T(128)}, u32[]{:S(2)}) copy-start(s32[32]{0:T(128)} %param.11) | copy-start | bytes 388
  0.6 14.6 %copy-start.1 = (s32[32]{0:T(128)S(1)}, s32[32]{0:T(128)}, u32[]{:S(2)}) copy-start(s32[32]{0:T(128)} %param.12) | copy-start | bytes 388
  15.3 192.2 %copy-start = (s32[64]{0:T(128)S(1)}, s32[64]{0:T(128)}, u32[]{:S(2)}) copy-start(s32[64]{0:T(128)} %param.9) | copy-start | bytes 772
  62.8 144.3 %all-to-all-start = ((bf16[4,2,4096]{2,1,0:T(2,128)(2,1)}), bf16[4,2,4096]{2,1,0:T(2,128)(2,1)S(1)}, u32[]{:S(2)}, u32[]{:S(2)}) async-start(bf16[4,2,4096]{2,1,0:T(2,128)(2,1)} %reshape.63), calls=%async_computation | async-start | bytes 131072 | tf_op jit(solution)/shard_map/all_to_all | solution.py:66
where the time goes:
time: 411 us; the launch traced here: 408 us
  blocking collectives  164 us (40%)
  starting transfers between devices  139 us (34%)
  loops' own time  61.1 us (15%)
  other arithmetic  29.4 us (7%)
  local copies, waits for them, and re-layouts  8.18 us (2%)
  waiting for transfers between devices  5.74 us (1%)
    all_to_all x1, blocking collectives, per_device(): lax.all_to_all(partial_value.reshape(sources_all, 1, n_col * width), 'col...  141 us
    all_to_all x1, starting transfers between devices, per_device(): lax.all_to_all(partial_value.reshape(sources_all, 1, n_col * width), 'col...  139 us
    another operation x2, loops' own time, relax_tiles(): return lax.fori_loop(0, (live_total + 3) // 4, relax_four, partial_value)  61.1 us
    reduce_min x16, other arithmetic, relax_four(): candidate = jnp.min(source[:, :, None] + weight[None, :, :], axis=1)  21.9 us
    all_gather x2, blocking collectives, per_device(): gathered = lax.all_gather(dist, ('row', 'rep'), axis=1, tiled=True)  19.6 us
  transfers between devices with their start and end apart: 1, of which 1 were waited for; matrix products, arithmetic and copies ran while one was open for 0% of the time, Pallas kernels for 0%

commit v1 on v0

v1 whole, which is shorter than its diff:
```python
import functools

import jax
import jax.numpy as jnp
from jax import lax
from jax.experimental import pallas as pl
from jax.experimental.pallas import tpu as pltpu
from jax.sharding import PartitionSpec as P

BLK_DEV = 1
STEP = 7.5
HALF = 63.0
FAR = 255.0
CHUNKS = 4


def first_kernel(n_row, n_col, n_rep, src, dst, count, sources, weights, code, part, hot, best, raw, sems):
    tiles, size, _ = code.shape
    height = hot.shape[1]
    step = tiles // CHUNKS
    copies = [
        pltpu.make_async_copy(
            weights.at[pl.ds(c * step, step)], raw.at[pl.ds(c * step, step)], sems.at[c]
        )
        for c in range(CHUNKS)
    ]
    for copy in copies:
        copy.start()
    col = lax.axis_index("col")
    wanted = jnp.broadcast_to(sources[...], (size, height)).T
    lane = lax.broadcasted_iota(jnp.int32, (height, size), 1)
    for q in range(n_row * n_rep):
        block = ((q // n_rep) * n_col + col) * n_rep + q % n_rep
        hot[q] = jnp.where(wanted == lane + block * size, 2.0**HALF, 0.0).astype(jnp.bfloat16)
    best[...] = jnp.zeros_like(best)
    live = count[0]
    for c, copy in enumerate(copies):
        copy.wait()
        for k in range(c * step, (c + 1) * step):
            w = raw[k].astype(jnp.float32)
            bound = jnp.where(k < live, 0.5, 1e9)
            coded = jnp.where(w > bound, jnp.exp2(HALF - STEP * w), 0.0).astype(jnp.bfloat16)
            code[k] = coded
            piece = src[k] // BLK_DEV
            q = piece // (n_col * n_rep) * n_rep + lax.rem(piece, n_rep)
            total = jnp.dot(hot[q], coded, preferred_element_type=jnp.float32)
            d = lax.rem(dst[k] // BLK_DEV // n_rep, n_col)
            best[d] = jnp.maximum(best[d], total)
    part[...] = (best[...] * 2.0**-HALF).astype(jnp.bfloat16)


def second_kernel(n_row, n_col, n_rep, src, dst, dist, code, part, best):
    best[...] = jnp.zeros_like(best)
    for k in range(code.shape[0]):
        piece = src[k] // BLK_DEV
        q = piece // (n_col * n_rep) * n_rep + lax.rem(piece, n_rep)
        total = jnp.dot(dist[q], code[k], preferred_element_type=jnp.float32)
        d = lax.rem(dst[k] // BLK_DEV // n_rep, n_col)
        best[d] = jnp.maximum(best[d], total)
    part[...] = best[...].astype(jnp.bfloat16)


def final_kernel(fresh, own, distances, sums):
    best = jnp.max(fresh[...].astype(jnp.float32), axis=0)
    best = jnp.maximum(best, own[...].astype(jnp.float32) * 2.0**HALF)
    level = jnp.ceil((2 * HALF - 0.22 - jnp.log2(jnp.maximum(best, 2.0**-125))) / STEP)
    value = jnp.where(best > 0.0, level, FAR)
    distances[...] = value
    inverse = jnp.where(value > 0.0, 1.0 / jnp.maximum(value, 1.0), 0.0)
    sums[...] = jnp.sum(inverse.T, axis=0, keepdims=True)


def per_device(sources, tile_weights, tile_src, tile_dst, tile_count):
    n_row, n_col, n_rep = (lax.axis_size(a) for a in ("row", "col", "rep"))
    height = sources.shape[0]
    tiles, size, _ = tile_weights.shape
    smem = pl.BlockSpec(memory_space=pltpu.SMEM)
    vmem = pl.BlockSpec(memory_space=pltpu.VMEM)
    sizes = (n_row, n_col, n_rep)
    code, part = pl.pallas_call(
        functools.partial(first_kernel, *sizes),
        out_shape=(
            jax.ShapeDtypeStruct((tiles, size, size), jnp.bfloat16),
            jax.ShapeDtypeStruct((n_col, height, size), jnp.bfloat16),
        ),
        in_specs=[smem, smem, smem, vmem, pl.BlockSpec(memory_space=pl.ANY)],
        out_specs=(vmem, vmem),
        scratch_shapes=[
            pltpu.VMEM((n_row * n_rep, height, size), jnp.bfloat16),
            pltpu.VMEM((n_col, height, size), jnp.float32),
            pltpu.VMEM((tiles, size, size), jnp.int32),
            pltpu.SemaphoreType.DMA((CHUNKS,)),
        ],
        name="round_one",
    )(tile_src, tile_dst, tile_count, sources.reshape(1, height), tile_weights)
    piece = (lax.axis_index("row") * n_col + lax.axis_index("col")) * n_rep + lax.axis_index("rep")
    columns = piece * size + jnp.arange(size, dtype=jnp.int32)
    start = jnp.where(columns[None, :] == sources[:, None], 2.0**HALF, 0.0).astype(jnp.bfloat16)
    fresh = lax.all_to_all(part, "col", 0, 0)
    own = jnp.maximum(jnp.max(fresh, axis=0), start)
    dist = lax.all_gather(own, ("row", "rep"), axis=0)
    part = pl.pallas_call(
        functools.partial(second_kernel, *sizes),
        out_shape=jax.ShapeDtypeStruct((n_col, height, size), jnp.bfloat16),
        in_specs=[smem, smem, vmem, vmem],
        out_specs=vmem,
        scratch_shapes=[pltpu.VMEM((n_col, height, size), jnp.float32)],
        name="round_two",
    )(tile_src, tile_dst, dist, code)
    fresh = lax.all_to_all(part, "col", 0, 0)
    distances, sums = pl.pallas_call(
        final_kernel,
        out_shape=(
            jax.ShapeDtypeStruct((height, size), jnp.float32),
            jax.ShapeDtypeStruct((1, height), jnp.float32),
        ),
        in_specs=[vmem, vmem],
        out_specs=(vmem, vmem),
        name="decode",
    )(fresh, own)
    other = lax.ppermute(sums, "rep", [(i, i ^ 1) for i in range(n_rep)])
    return distances, sums + other


def solution(mesh):
    cut = ("row", "col", "rep")
    return jax.shard_map(
        per_device,
        mesh=mesh,
        in_specs=(P(), P(cut, None, None), P(cut), P(cut), P(cut)),
        out_specs=(P(None, cut), P(("row", "col"), None)),
        check_vma=False,
    )
```

time: 411 us -> 44 us (0.11)
  blocking collectives: 164 us -> 10.2 us
  starting transfers between devices: 139 us -> 9.64 us
  loops' own time: 61.1 us -> 0 us
  other arithmetic: 29.4 us -> 1.95 us
  Pallas kernels: 0 us -> 7.65 us
  local copies, waits for them, and re-layouts: 8.18 us -> 0.63 us
  waiting for transfers between devices: 5.74 us -> 12.1 us
    all_to_all x1 -> x0, blocking collectives: 141 us -> none  [per_device(): lax.all_to_all(partial_value.reshape(sources_all, 1, n_col * width), 'col...]
    all_to_all x1 -> x2, starting transfers between devices: 139 us -> 9.64 us  [per_device(): fresh = lax.all_to_all(part, 'col', 0, 0)]
    another operation x2 -> x0, loops' own time: 61.1 us -> none  [relax_tiles(): return lax.fori_loop(0, (live_total + 3) // 4, relax_four, partial_value)]
    reduce_min x18 -> x0, other arithmetic: 22.1 us -> none  [the longest x16 21.9 us: relax_four(): candidate = jnp.min(source[:, :, None] + weight[None, :, :], axis=1)]
    all_gather x2 -> x1, blocking collectives: 19.6 us -> 10.2 us  [per_device(): dist = lax.all_gather(own, ('row', 'rep'), axis=0)]
    pallas_call x0 -> x3, Pallas kernels: none -> 7.65 us  [the longest x1 3.73 us: per_device(): pl.pallas_call(functools.partial(first_kernel, *sizes), out_shape=(jax.Sh...]
    dynamic_slice x12 -> x0, local copies, waits for them, and re-layouts: 5.69 us -> none  [the longest x8 2.94 us: relax_four(): source = lax.dynamic_slice_in_dim(gathered, src_pos[picked] * BS, BS, 1)]
    all_to_all x1 -> x2, waiting for transfers between devices: 5.74 us -> 10.8 us  [per_device(): fresh = lax.all_to_all(part, 'col', 0, 0)]
  transfers between devices with their start and end apart: 1 -> 3, of which waited for: 1 -> 3; matrix products, arithmetic and copies ran while one was open for 0% -> 2% of each run, Pallas kernels for 0% -> 0%
where the time goes in v1:
time: 44 us; the launch traced here: 43.5 us
  waiting for transfers between devices  12.1 us (28%)
  blocking collectives  10.2 us (23%)
  starting transfers between devices  9.64 us (22%)
  Pallas kernels  7.65 us (17%)
  other arithmetic  1.95 us (4%)
  between operations  1.33 us (3%)
  local copies, waits for them, and re-layouts  0.63 us (1%)
    all_to_all x2, waiting for transfers between devices, per_device(): fresh = lax.all_to_all(part, 'col', 0, 0)  10.8 us
    all_gather x1, blocking collectives, per_device(): dist = lax.all_gather(own, ('row', 'rep'), axis=0)  10.2 us
    all_to_all x2, starting transfers between devices, per_device(): fresh = lax.all_to_all(part, 'col', 0, 0)  9.64 us
    pallas_call x1, Pallas kernels, per_device(): pl.pallas_call(functools.partial(first_kernel, *sizes), out_shape=(jax.Sh...  3.73 us
    pallas_call x1, Pallas kernels, per_device(): pl.pallas_call(functools.partial(second_kernel, *sizes), out_shape=jax.Sh...  2.43 us
    pallas_call x1, Pallas kernels, per_device(): pl.pallas_call(final_kernel, out_shape=(jax.ShapeDtypeStruct((height, siz...  1.49 us
    ppermute x1, waiting for transfers between devices, per_device(): other = lax.ppermute(sums, 'rep', [(i, i ^ 1) for i in range(n_rep)])  1.29 us
    add x1, other arithmetic, per_device(): return (distances, sums + other)  1.17 us
  transfers between devices with their start and end apart: 3, of which 3 were waited for; matrix products, arithmetic and copies ran while one was open for 2% of the time, Pallas kernels for 0%

profile of v1, /device:TPU:0, one launch (start us, length us, event | category | flops | bytes accessed | tf_op | source)
XLA Modules:
  0.0 43.5 jit_solution(15587222685323949050)
XLA Ops:
  0.6 0.0 copy-start.1
  1.3 3.7 %round_one.1 = (bf16[32,128,128]{2,1,0:T(8,128)(2,1)}, bf16[4,64,128]{2,1,0:T(8,128)(2,1)}) custom-call(s32[32]{0:T(128)} %src.3, s32[32]{0:T(128)} %dst.3, s32[1]{0:T(128)S(6)} %copy.7.count, s32[1,64]{1,0:T(1,128)} %bitcast.3, s32[32,128,128]{2,1,0:T(8,128)} %weights.1), custom_call_target="tpu_custom_call" | custom-call | tf_op jit(solution)/shard_map/round_one/pallas_call | solution.py:80
  5.0 6.4 %all-to-all-start = ((bf16[4,64,128]{2,1,0:T(8,128)(2,1)}), bf16[4,64,128]{2,1,0:T(8,128)(2,1)S(1)}, u32[]{:S(2)}, u32[]{:S(2)}) async-start(bf16[4,64,128]{2,1,0:T(8,128)(2,1)} %get-tuple-element.6), calls=%async_computation | async-start | bytes 131072 | tf_op jit(solution)/shard_map/all_to_all | solution.py:99
  11.4 5.7 %all-to-all-done = bf16[4,64,128]{2,1,0:T(8,128)(2,1)S(1)} async-done(((bf16[4,64,128]{2,1,0:T(8,128)(2,1)}), bf16[4,64,128]{2,1,0:T(8,128)(2,1)S(1)}, u32[]{:S(2)}, u32[]{:S(2)}) %all-to-all-start) | async-done | bytes 65568 | tf_op jit(solution)/shard_map/all_to_all | solution.py:99
  17.2 0.0 copy-done.1
  17.2 0.1 fusion
  17.2 10.2 %all_gather.4.dist = bf16[8,64,128]{2,1,0:T(8,128)(2,1)} all-gather(bf16[1,64,128]{2,1,0:T(8,128)(2,1)S(1)} %fusion), channel_id=1, replica_groups=mesh['row'=4,'col'=4,'rep'=2] {'row','rep'}, dimensions={0}, use_global_device_ids=true | all-gather | bytes 147456 | tf_op jit(solution)/shard_map/all_gather | solution.py:101
  27.5 2.4 %round_two.1 = bf16[4,64,128]{2,1,0:T(8,128)(2,1)} custom-call(s32[32]{0:T(128)} %src.3, s32[32]{0:T(128)} %dst.3, bf16[8,64,128]{2,1,0:T(8,128)(2,1)} %all_gather.4.dist, bf16[32,128,128]{2,1,0:T(8,128)(2,1)} %get-tuple-element.7.code), custom_call_target="tpu_custom_call" | custom-call | tf_op jit(solution)/shard_map/round_two/pallas_call | solution.py:102
  29.9 3.3 %all-to-all-start.1 = ((bf16[4,64,128]{2,1,0:T(8,128)(2,1)}), bf16[4,64,128]{2,1,0:T(8,128)(2,1)S(1)}, u32[]{:S(2)}, u32[]{:S(2)}) async-start(bf16[4,64,128]{2,1,0:T(8,128)(2,1)} %round_two.1), calls=%async_computation.1 | async-start | bytes 131072 | tf_op jit(solution)/shard_map/all_to_all | solution.py:110
  33.2 0.7 %fusion.1.own = bf16[64,128]{1,0:T(8,128)(2,1)} fusion(bf16[64,128]{1,0:T(8,128)(2,1)S(1)} %reduce_max.11, s32[128]{0:T(128)S(1)} %iota_add_fusion, s32[64]{0:T(128)S(1)} %copy-done.1), kind=kLoop, calls=%fused_computation.3 | loop fusion | flops 32768 | bytes 33536 | tf_op jit(solution)/shard_map/max | solution.py:100
  33.9 5.0 %all-to-all-done.1.fresh = bf16[4,64,128]{2,1,0:T(8,128)(2,1)S(1)} async-done(((bf16[4,64,128]{2,1,0:T(8,128)(2,1)}), bf16[4,64,128]{2,1,0:T(8,128)(2,1)S(1)}, u32[]{:S(2)}, u32[]{:S(2)}) %all-to-all-start.1) | async-done | bytes 65568 | tf_op jit(solution)/shard_map/all_to_all | solution.py:110
  38.9 0.0 copy-start
  38.9 0.6 %copy-done = bf16[4,64,128]{2,1,0:T(8,128)(2,1)} copy-done((bf16[4,64,128]{2,1,0:T(8,128)(2,1)}, bf16[4,64,128]{2,1,0:T(8,128)(2,1)S(1)}, u32[]{:S(2)}) %copy-start) | copy-done | bytes 65560
  39.6 1.5 %decode.1 = (f32[64,128]{1,0:T(8,128)}, f32[1,64]{1,0:T(1,128)}) custom-call(bf16[4,64,128]{2,1,0:T(8,128)(2,1)} %copy-done, bf16[64,128]{1,0:T(8,128)(2,1)} %fusion.1.own), custom_call_target="tpu_custom_call" | custom-call | tf_op jit(solution)/shard_map/decode/pallas_call | solution.py:111
  41.0 0.0 collective-permute-start
  41.0 1.3 %collective-permute-done = f32[1,64]{1,0:T(1,128)S(1)} collective-permute-done((f32[1,64]{1,0:T(1,128)}, f32[1,64]{1,0:T(1,128)S(1)}, u32[]{:S(2)}, u32[]{:S(2)}) %collective-permute-start) | collective-permute-done | bytes 288 | tf_op jit(solution)/shard_map/ppermute | solution.py:121
  42.3 1.2 %add.23 = f32[1,64]{1,0:T(1,128)} add(f32[1,64]{1,0:T(1,128)} %get-tuple-element.9, f32[1,64]{1,0:T(1,128)S(1)} %collective-permute-done) | non-fusion elementwise | flops 64 | bytes 768 | tf_op jit(solution)/shard_map/add | solution.py:122
  (2 shorter events, 0.0 us)
Async XLA Ops:
  0.6 16.5 %copy-start.1 = (s32[64]{0:T(128)S(1)}, s32[64]{0:T(128)}, u32[]{:S(2)}) copy-start(s32[64]{0:T(128)} %param.5) | copy-start | bytes 772
  5.0 12.1 %all-to-all-start = ((bf16[4,64,128]{2,1,0:T(8,128)(2,1)}), bf16[4,64,128]{2,1,0:T(8,128)(2,1)S(1)}, u32[]{:S(2)}, u32[]{:S(2)}) async-start(bf16[4,64,128]{2,1,0:T(8,128)(2,1)} %get-tuple-element.6), calls=%async_computation | async-start | bytes 131072 | tf_op jit(solution)/shard_map/all_to_all | solution.py:99
  29.9 9.0 %all-to-all-start.1 = ((bf16[4,64,128]{2,1,0:T(8,128)(2,1)}), bf16[4,64,128]{2,1,0:T(8,128)(2,1)S(1)}, u32[]{:S(2)}, u32[]{:S(2)}) async-start(bf16[4,64,128]{2,1,0:T(8,128)(2,1)} %round_two.1), calls=%async_computation.1 | async-start | bytes 131072 | tf_op jit(solution)/shard_map/all_to_all | solution.py:110
  38.9 0.6 %copy-start = (bf16[4,64,128]{2,1,0:T(8,128)(2,1)}, bf16[4,64,128]{2,1,0:T(8,128)(2,1)S(1)}, u32[]{:S(2)}) copy-start(bf16[4,64,128]{2,1,0:T(8,128)(2,1)S(1)} %all-to-all-done.1.fresh) | copy-start | bytes 196612
  41.0 1.3 %collective-permute-start = (f32[1,64]{1,0:T(1,128)}, f32[1,64]{1,0:T(1,128)S(1)}, u32[]{:S(2)}, u32[]{:S(2)}) collective-permute-start(f32[1,64]{1,0:T(1,128)} %get-tuple-element.9), channel_id=1, source_target_pairs={{0,1},{1,0},{2,3},{3,2},{4,5},{5,4},{6,7},{7,6},{8,9},{9,8},{10,11... | collective-permute-start | bytes 776 | tf_op jit(solution)/shard_map/ppermute | solution.py:121

commit v2 on v1

v2 whole, which is shorter than its diff:
```python
import functools

import jax
import jax.numpy as jnp
from jax import lax
from jax.experimental import pallas as pl
from jax.experimental.pallas import tpu as pltpu
from jax.sharding import PartitionSpec as P

BLK_DEV = 1
STEP = 7.5
HALF = 63.0
FAR = 255.0
CHUNKS = 8


def relax(dist, edges, best):
    for q in range(dist.shape[0]):
        left = dist[q]
        for d in range(best.shape[0]):
            total = jnp.dot(left, edges[q, d], preferred_element_type=jnp.float32)
            best[d] = total if q == 0 else jnp.maximum(best[d], total)


def first_kernel(n_row, n_col, n_rep, sources, weights, src, dst, count, edges, hot, part, best, raw, ids, s_src, s_dst, sems, small):
    tiles, size, _ = raw.shape
    height = hot.shape[1]
    step = tiles // CHUNKS
    firsts = [
        pltpu.make_async_copy(a, b, small.at[i])
        for i, (a, b) in enumerate(((sources, ids), (src, s_src), (dst, s_dst)))
    ]
    for copy in firsts:
        copy.start()
    copies = [
        pltpu.make_async_copy(
            weights.at[pl.ds(c * step, step)], raw.at[pl.ds(c * step, step)], sems.at[c]
        )
        for c in range(CHUNKS)
    ]
    for copy in copies:
        copy.start()
    edges[...] = jnp.zeros_like(edges)
    for copy in firsts:
        copy.wait()
    col = lax.axis_index("col")
    wanted = jnp.broadcast_to(ids[...], (size, height)).T
    lane = lax.broadcasted_iota(jnp.int32, (height, size), 1)
    for q in range(n_row * n_rep):
        block = ((q // n_rep) * n_col + col) * n_rep + q % n_rep
        hot[q] = jnp.where(wanted == lane + block * size, 2.0**HALF, 0.0).astype(jnp.bfloat16)
    live = count[0]
    for c, copy in enumerate(copies):
        copy.wait()
        for k in range(c * step, (c + 1) * step):
            w = raw[k].astype(jnp.float32)
            bound = jnp.where(k < live, 0.5, 1e9)
            coded = jnp.where(w > bound, jnp.exp2(HALF - STEP * w), 0.0).astype(jnp.bfloat16)
            piece = s_src[k] // BLK_DEV
            q = piece // (n_col * n_rep) * n_rep + lax.rem(piece, n_rep)
            d = lax.rem(s_dst[k] // BLK_DEV // n_rep, n_col)
            edges[q, d] = jnp.maximum(edges[q, d], coded)
    relax(hot, edges, best)
    coded = (best[...] * 2.0**-HALF).astype(jnp.bfloat16)
    for r in range(n_row):
        part[r] = coded


def second_kernel(n_row, n_col, n_rep, mine, other, hot, edges, part, own, dist, best):
    rep = lax.axis_index("rep")
    for r in range(n_row):
        for p in range(n_rep):
            got = jnp.where(rep == p, jnp.max(mine[r], axis=0), jnp.max(other[r], axis=0))
            dist[r * n_rep + p] = jnp.maximum(got, hot[r * n_rep + p])
    own[...] = dist[lax.axis_index("row") * n_rep + rep]
    relax(dist, edges, best)
    part[...] = best[...].astype(jnp.bfloat16)


def final_kernel(fresh, own, distances, sums):
    best = jnp.max(fresh[...].astype(jnp.float32), axis=0)
    best = jnp.maximum(best, own[...].astype(jnp.float32) * 2.0**HALF)
    level = jnp.ceil((2 * HALF - 0.22 - jnp.log2(jnp.maximum(best, 2.0**-125))) / STEP)
    value = jnp.where(best > 0.0, level, FAR)
    distances[...] = jnp.where(value > 0.0, value, 0.0)
    inverse = jnp.where(value > 0.0, 1.0 / jnp.maximum(value, 1.0), 0.0)
    sums[...] = jnp.sum(inverse.T, axis=0, keepdims=True)


def in_hbm(array):
    return pltpu.with_memory_space_constraint(array, pltpu.HBM)


def per_device(sources, tile_weights, tile_src, tile_dst, tile_count):
    n_row, n_col, n_rep = (lax.axis_size(a) for a in ("row", "col", "rep"))
    height = sources.shape[0]
    tiles, size, _ = tile_weights.shape
    slots = n_row * n_rep
    vmem = pl.BlockSpec(memory_space=pltpu.VMEM)
    hbm = pl.BlockSpec(memory_space=pltpu.HBM)
    sizes = (n_row, n_col, n_rep)
    limit = pltpu.CompilerParams(vmem_limit_bytes=12 << 20)
    edges, hot, part = pl.pallas_call(
        functools.partial(first_kernel, *sizes),
        out_shape=(
            jax.ShapeDtypeStruct((slots, n_col, size, size), jnp.bfloat16),
            jax.ShapeDtypeStruct((slots, height, size), jnp.bfloat16),
            jax.ShapeDtypeStruct((n_row, n_col, height, size), jnp.bfloat16),
        ),
        in_specs=[hbm] * 4 + [pl.BlockSpec(memory_space=pltpu.SMEM)],
        out_specs=(vmem,) * 3,
        scratch_shapes=[
            pltpu.VMEM((n_col, height, size), jnp.float32),
            pltpu.VMEM((tiles, size, size), jnp.int32),
            pltpu.VMEM((1, height), jnp.int32),
            pltpu.SMEM((tiles,), jnp.int32),
            pltpu.SMEM((tiles,), jnp.int32),
            pltpu.SemaphoreType.DMA((CHUNKS,)),
            pltpu.SemaphoreType.DMA((3,)),
        ],
        compiler_params=limit,
        name="round_one",
    )(*map(in_hbm, (sources.reshape(1, height), tile_weights, tile_src, tile_dst)), tile_count)
    mine = lax.all_to_all(
        part.reshape(n_row * n_col, height, size), ("row", "col"), 0, 0
    ).reshape(n_row, n_col, height, size)
    other = lax.ppermute(mine, "rep", [(i, (i + 1) % n_rep) for i in range(n_rep)])
    part, own = pl.pallas_call(
        functools.partial(second_kernel, *sizes),
        out_shape=(
            jax.ShapeDtypeStruct((n_col, height, size), jnp.bfloat16),
            jax.ShapeDtypeStruct((height, size), jnp.bfloat16),
        ),
        in_specs=[vmem] * 4,
        out_specs=(vmem,) * 2,
        scratch_shapes=[
            pltpu.VMEM((slots, height, size), jnp.bfloat16),
            pltpu.VMEM((n_col, height, size), jnp.float32),
        ],
        compiler_params=limit,
        name="round_two",
    )(mine, other, hot, edges)
    fresh = lax.all_to_all(part, "col", 0, 0)
    distances, sums = pl.pallas_call(
        final_kernel,
        out_shape=(
            jax.ShapeDtypeStruct((height, size), jnp.float32),
            jax.ShapeDtypeStruct((1, height), jnp.float32),
        ),
        in_specs=[vmem, vmem],
        out_specs=(vmem, vmem),
        compiler_params=limit,
        name="decode",
    )(fresh, own)
    other = lax.ppermute(sums, "rep", [(i, (i + 1) % n_rep) for i in range(n_rep)])
    return distances, sums + other


def solution(mesh):
    cut = ("row", "col", "rep")
    return jax.shard_map(
        per_device,
        mesh=mesh,
        in_specs=(P(), P(cut, None, None), P(cut), P(cut), P(cut)),
        out_specs=(P(None, cut), P(("row", "col"), None)),
        check_vma=False,
    )
```

time: 44 us -> 34.9 us (0.79)
  blocking collectives: 10.2 us -> 26.8 us
  starting transfers between devices: 9.64 us -> 0.01 us
  waiting for transfers between devices: 12.1 us -> 2.69 us
  Pallas kernels: 7.65 us -> 3.38 us
  other arithmetic: 1.95 us -> 0.51 us
  local copies, waits for them, and re-layouts: 0.63 us -> 0 us
    all_to_all x0 -> x2, blocking collectives: none -> 26.8 us  [the longest x1 18.7 us: per_device(): lax.all_to_all(part.reshape(n_row * n_col, height, size), ('row', 'col'),...]
    all_to_all x2 -> x0, waiting for transfers between devices: 10.8 us -> none  [per_device(): fresh = lax.all_to_all(part, 'col', 0, 0)]
    all_gather x1 -> x0, blocking collectives: 10.2 us -> none  [per_device(): dist = lax.all_gather(own, ('row', 'rep'), axis=0)]
    all_to_all x2 -> x0, starting transfers between devices: 9.64 us -> none  [per_device(): fresh = lax.all_to_all(part, 'col', 0, 0)]
    pallas_call x1, Pallas kernels: 2.43 us -> 0.42 us  [per_device(): pl.pallas_call(functools.partial(second_kernel, *sizes), out_shape=(jax.S...]
    pallas_call x1, Pallas kernels: 3.73 us -> 2.31 us  [per_device(): pl.pallas_call(functools.partial(first_kernel, *sizes), out_shape=(jax.Sh...]
    ppermute x1 -> x2, waiting for transfers between devices: 1.29 us -> 2.69 us  [the longest x1 1.53 us: per_device(): lax.ppermute(mine, 'rep', [(i, (i + 1) % n_rep) for i in range(n_rep)])]
    pallas_call x1, Pallas kernels: 1.49 us -> 0.64 us  [per_device(): pl.pallas_call(final_kernel, out_shape=(jax.ShapeDtypeStruct((height, siz...]
  transfers between devices with their start and end apart: 3 -> 2, of which waited for: 3 -> 2; matrix products, arithmetic and copies ran while one was open for 2% -> 0% of each run, Pallas kernels for 0% -> 0%
where the time goes in v2:
time: 34.9 us; the launch traced here: 34.7 us
  blocking collectives  26.8 us (77%)
  Pallas kernels  3.38 us (10%)
  waiting for transfers between devices  2.69 us (8%)
  between operations  1.3 us (4%)
  other arithmetic  0.51 us (1%)
    all_to_all x1, blocking collectives, per_device(): lax.all_to_all(part.reshape(n_row * n_col, height, size), ('row', 'col'),...  18.7 us
    all_to_all x1, blocking collectives, per_device(): fresh = lax.all_to_all(part, 'col', 0, 0)  8.11 us
    pallas_call x1, Pallas kernels, per_device(): pl.pallas_call(functools.partial(first_kernel, *sizes), out_shape=(jax.Sh...  2.31 us
    ppermute x1, waiting for transfers between devices, per_device(): lax.ppermute(mine, 'rep', [(i, (i + 1) % n_rep) for i in range(n_rep)])  1.53 us
    ppermute x1, waiting for transfers between devices, per_device(): lax.ppermute(sums, 'rep', [(i, (i + 1) % n_rep) for i in range(n_rep)])  1.16 us
  transfers between devices with their start and end apart: 2, of which 2 were waited for; matrix products, arithmetic and copies ran while one was open for 0% of the time, Pallas kernels for 0%

profile of v2, /device:TPU:0, one launch (start us, length us, event | category | flops | bytes accessed | tf_op | source)
XLA Modules:
  0.0 34.7 jit_solution(15829214793371957722)
XLA Ops:
  1.3 2.3 %round_one.1 = (bf16[8,4,128,128]{3,2,1,0:T(8,128)(2,1)S(1)}, bf16[8,64,128]{2,1,0:T(8,128)(2,1)S(1)}, bf16[4,4,64,128]{3,2,1,0:T(8,128)(2,1)S(1)}) custom-call(s32[1,64]{1,0:T(1,128)} %bitcast.6, s32[32,128,128]{2,1,0:T(8,128)} %weights.1, s32[32]{0:T(128)} %src.1, s32[32]{0:T(128)} %dst.1, s32[1]{0:T(128)S(6)} %copy.7.count), custom_call_target="tpu_custom_call" | custom-call | tf_op jit(solution)/shard_map/round_one/pallas_call | solution.py:103
  3.6 18.7 %all_to_all.10 = bf16[16,64,128]{2,1,0:T(8,128)(2,1)S(1)} all-to-all(bf16[16,64,128]{2,1,0:T(8,128)(2,1)S(1)} %bitcast.5), channel_id=1, replica_groups=mesh['row'=4,'col'=4,'rep'=2] {'row','col'}, dimensions={0} | all-to-all | bytes 524288 | tf_op jit(solution)/shard_map/all_to_all | solution.py:124
  22.3 0.0 collective-permute-start
  22.3 1.5 %collective-permute-done.other = bf16[4,4,64,128]{3,2,1,0:T(8,128)(2,1)S(1)} collective-permute-done((bf16[4,4,64,128]{3,2,1,0:T(8,128)(2,1)S(1)}, bf16[4,4,64,128]{3,2,1,0:T(8,128)(2,1)S(1)}, u32[]{:S(2)}, u32[]{:S(2)}) %collective-permute-start) | collective-permute-done | bytes 262176 | tf_op jit(solution)/shard_map/ppermute | solution.py:127
  23.8 0.4 %round_two.1 = (bf16[4,64,128]{2,1,0:T(8,128)(2,1)S(1)}, bf16[64,128]{1,0:T(8,128)(2,1)S(1)}) custom-call(bf16[4,4,64,128]{3,2,1,0:T(8,128)(2,1)S(1)} %bitcast.4, bf16[4,4,64,128]{3,2,1,0:T(8,128)(2,1)S(1)} %collective-permute-done.other, bf16[8,64,128]{2,1,0:T(8,128)(2,1)S(1)} %get-tuple-element.10.hot, bf16[8,4,128,128]{3,2,1,0:T(8,128)(2,1)S(1)} %get-tuple-element.11.edges), custom_call_target="tpu_custom_call" | custom-call | tf_op jit(solution)/shard_map/round_two/pallas_call | solution.py:128
  24.3 8.1 %all_to_all.11.fresh = bf16[4,64,128]{2,1,0:T(8,128)(2,1)S(1)} all-to-all(bf16[4,64,128]{2,1,0:T(8,128)(2,1)S(1)} %get-tuple-element.12), channel_id=1, replica_groups=mesh['row'=4,'col'=4,'rep'=2] {'col'}, dimensions={0} | all-to-all | bytes 131072 | tf_op jit(solution)/shard_map/all_to_all | solution.py:143
  32.4 0.6 %decode.1 = (f32[64,128]{1,0:T(8,128)}, f32[1,64]{1,0:T(1,128)S(1)}) custom-call(bf16[4,64,128]{2,1,0:T(8,128)(2,1)S(1)} %all_to_all.11.fresh, bf16[64,128]{1,0:T(8,128)(2,1)S(1)} %get-tuple-element.13.own), custom_call_target="tpu_custom_call" | custom-call | tf_op jit(solution)/shard_map/decode/pallas_call | solution.py:144
  33.0 0.0 collective-permute-start.1
  33.0 1.2 %collective-permute-done.1 = f32[1,64]{1,0:T(1,128)S(1)} collective-permute-done((f32[1,64]{1,0:T(1,128)S(1)}, f32[1,64]{1,0:T(1,128)S(1)}, u32[]{:S(2)}, u32[]{:S(2)}) %collective-permute-start.1) | collective-permute-done | bytes 288 | tf_op jit(solution)/shard_map/ppermute | solution.py:155
  34.2 0.5 %add.3 = f32[1,64]{1,0:T(1,128)} add(f32[1,64]{1,0:T(1,128)S(1)} %get-tuple-element.15, f32[1,64]{1,0:T(1,128)S(1)} %collective-permute-done.1) | non-fusion elementwise | flops 64 | bytes 768 | tf_op jit(solution)/shard_map/add | solution.py:156
Async XLA Ops:
  22.3 1.5 %collective-permute-start = (bf16[4,4,64,128]{3,2,1,0:T(8,128)(2,1)S(1)}, bf16[4,4,64,128]{3,2,1,0:T(8,128)(2,1)S(1)}, u32[]{:S(2)}, u32[]{:S(2)}) collective-permute-start(bf16[4,4,64,128]{3,2,1,0:T(8,128)(2,1)S(1)} %bitcast.3), channel_id=1, source_target_pairs={{0,1},{1,0},{2,3},{3,2},{4,5},{5,4},{6,7},{7,6},{8,9},{9,8},{10,11... | collective-permute-start | bytes 786440 | tf_op jit(solution)/shard_map/ppermute | solution.py:127
  33.0 1.2 %collective-permute-start.1 = (f32[1,64]{1,0:T(1,128)S(1)}, f32[1,64]{1,0:T(1,128)S(1)}, u32[]{:S(2)}, u32[]{:S(2)}) collective-permute-start(f32[1,64]{1,0:T(1,128)S(1)} %get-tuple-element.15), channel_id=1, source_target_pairs={{0,1},{1,0},{2,3},{3,2},{4,5},{5,4},{6,7},{7,6},{8,9},{9,8},{10,11... | collective-permute-start | bytes 776 | tf_op jit(solution)/shard_map/ppermute | solution.py:155

commit v3 on v2

v3 whole, which is shorter than its diff:
```python
import functools

import jax
import jax.numpy as jnp
from jax import lax
from jax.experimental import pallas as pl
from jax.experimental.pallas import tpu as pltpu
from jax.sharding import PartitionSpec as P

BLK_DEV = 1
STEP = 7.5
HALF = 63.0
FAR = 255.0
CHUNKS = 8
F32, BF16 = jnp.float32, jnp.bfloat16


def relax(dist, edges, best):
    for q in range(dist.shape[0]):
        left = dist[q]
        for d in range(best.shape[0]):
            total = jnp.dot(left, edges[q, d], preferred_element_type=F32)
            best[d] = total if q == 0 else jnp.maximum(best[d], total)


def column_of(vertex, size, n_col, n_rep):
    shift = (size * BLK_DEV * n_rep).bit_length() - 1
    return lax.shift_right_logical(vertex, shift) & (n_col - 1)


def spread(part, best):
    coded = (best[...] * 2.0**-HALF).astype(BF16)
    for r in range(part.shape[0]):
        part[r] = coded


def first_kernel(
    sizes, sources, weights, src, dst, count,
    edges, hot, pick, part, over,
    few, best, raw, ids, s_src, s_dst, sems, small,
):
    n_row, n_col, n_rep = sizes
    tiles, size, _ = raw.shape
    height, room = hot.shape[1], few.shape[1]
    step = tiles // CHUNKS
    firsts = [
        pltpu.make_async_copy(a, b, small.at[i])
        for i, (a, b) in enumerate(((sources, ids), (src, s_src), (dst, s_dst)))
    ]
    for copy in firsts:
        copy.start()
    copies = [
        pltpu.make_async_copy(
            weights.at[pl.ds(c * step, step)], raw.at[pl.ds(c * step, step)], sems.at[c]
        )
        for c in range(CHUNKS)
    ]
    for copy in copies:
        copy.start()
    edges[...] = jnp.zeros_like(edges)
    for copy in firsts:
        copy.wait()
    me = lax.axis_index("col")
    along = jnp.broadcast_to(ids[...], (size, height))
    down = along.T
    lane = lax.broadcasted_iota(jnp.int32, (height, size), 1)
    col_along = column_of(along[:height], size, n_col, n_rep)
    col_down = column_of(down, size, n_col, n_rep)
    s_a = lax.broadcasted_iota(jnp.int32, (height, height), 1)
    s_d = lax.broadcasted_iota(jnp.int32, (height, height), 0)
    same = col_along == col_down[:, :height]
    rank_down = jnp.sum(jnp.where(same & (s_a < s_d), 1.0, 0.0), axis=1, keepdims=True)
    rank_along = jnp.sum(jnp.where(same & (s_d < s_a), 1.0, 0.0), axis=0, keepdims=True)
    over[0] = (jnp.max(rank_along) >= room).astype(jnp.int32)
    place = lax.broadcasted_iota(jnp.int32, (height, n_col * room), 1)
    slot = jnp.where(rank_down < room, rank_down + room * col_down[:, :1].astype(F32), -1.0)
    pick[...] = jnp.where(place.astype(F32) == slot, 1.0, 0.0).astype(BF16)
    order = lax.broadcasted_iota(jnp.int32, (room, height), 0).astype(F32)
    taken = (order == rank_along) & (col_along[:room] == me)
    vertex = jnp.sum(jnp.where(taken, along[:room].astype(F32) + 1.0, 0.0), axis=1, keepdims=True) - 1.0
    for q in range(n_row * n_rep):
        at = lane + (((q // n_rep) * n_col + me) * n_rep + q % n_rep) * size
        hot[q] = jnp.where(down == at, 2.0**HALF, 0.0).astype(BF16)
        few[q] = jnp.where(vertex == at[:room].astype(F32), 2.0**HALF, 0.0).astype(BF16)
    live = count[0]
    for c, copy in enumerate(copies):
        copy.wait()
        for k in range(c * step, (c + 1) * step):
            w = raw[k].astype(F32).astype(BF16)
            bound = jnp.where(k < live, 0.5, 1e9).astype(BF16)
            coded = jnp.where(w > bound, jnp.exp2(BF16(HALF) - BF16(STEP) * w), BF16(0.0))
            piece = s_src[k] // BLK_DEV
            q = piece // (n_col * n_rep) * n_rep + lax.rem(piece, n_rep)
            d = lax.rem(s_dst[k] // BLK_DEV // n_rep, n_col)
            edges[q, d] = jnp.maximum(edges[q, d], coded)
    relax(few, edges, best)
    spread(part, best)


def first_kernel_all(hot, edges, part, best):
    relax(hot, edges, best)
    spread(part, best)


def second_kernel(sizes, packed, mine, other, hot, pick, edges, part, own, dist, best):
    n_row, n_col, n_rep = sizes
    rep = lax.axis_index("rep")
    for r in range(n_row):
        got = []
        for side in (mine, other):
            rows = side[r]
            if packed:
                rows = rows.reshape(-1, rows.shape[-1])
                got.append(jnp.dot(pick[...], rows, preferred_element_type=F32).astype(BF16))
            else:
                got.append(jnp.max(rows, axis=0))
        for p in range(n_rep):
            q = r * n_rep + p
            dist[q] = jnp.maximum(jnp.where(rep == p, got[0], got[1]), hot[q])
    own[...] = dist[lax.axis_index("row") * n_rep + rep]
    relax(dist, edges, best)
    part[...] = best[...].astype(BF16)


def final_kernel(fresh, own, distances, sums):
    best = jnp.max(fresh[...].astype(F32), axis=0)
    best = jnp.maximum(best, own[...].astype(F32) * 2.0**HALF)
    level = jnp.ceil((2 * HALF - 0.22 - jnp.log2(jnp.maximum(best, 2.0**-125))) / STEP)
    value = jnp.where(best > 0.0, level, FAR)
    distances[...] = jnp.where(value > 0.0, value, 0.0)
    inverse = jnp.where(value > 0.0, 1.0 / jnp.maximum(value, 1.0), 0.0)
    sums[...] = jnp.sum(inverse.T, axis=0, keepdims=True)


def in_hbm(array):
    return pltpu.with_memory_space_constraint(array, pltpu.HBM)


def per_device(sources, tile_weights, tile_src, tile_dst, tile_count):
    sizes = n_row, n_col, n_rep = tuple(lax.axis_size(a) for a in ("row", "col", "rep"))
    height = sources.shape[0]
    tiles, size, _ = tile_weights.shape
    slots = n_row * n_rep
    room = min(height, max(16, 2 * height // n_col))
    assert n_rep == 2 and all(n & (n - 1) == 0 for n in (*sizes, size))
    vmem = pl.BlockSpec(memory_space=pltpu.VMEM)
    smem = pl.BlockSpec(memory_space=pltpu.SMEM)
    hbm = pl.BlockSpec(memory_space=pltpu.HBM)
    limit = pltpu.CompilerParams(vmem_limit_bytes=14 << 20)
    shape = jax.ShapeDtypeStruct
    swap = [(i, (i + 1) % n_rep) for i in range(n_rep)]
    best = pltpu.VMEM((n_col, height, size), F32)
    edges, hot, pick, part, over = pl.pallas_call(
        functools.partial(first_kernel, sizes),
        out_shape=(
            shape((slots, n_col, size, size), BF16),
            shape((slots, height, size), BF16),
            shape((height, n_col * room), BF16),
            shape((n_row, n_col, room, size), BF16),
            pltpu.SMEM((1,), jnp.int32),
        ),
        in_specs=[hbm] * 4 + [smem],
        out_specs=(vmem,) * 4 + (smem,),
        scratch_shapes=[
            pltpu.VMEM((slots, room, size), BF16),
            pltpu.VMEM((n_col, room, size), F32),
            pltpu.VMEM((tiles, size, size), jnp.int32),
            pltpu.VMEM((1, height), jnp.int32),
            pltpu.SMEM((tiles,), jnp.int32),
            pltpu.SMEM((tiles,), jnp.int32),
            pltpu.SemaphoreType.DMA((CHUNKS,)),
            pltpu.SemaphoreType.DMA((3,)),
        ],
        compiler_params=limit,
        name="round_one",
    )(*map(in_hbm, (sources.reshape(1, height), tile_weights, tile_src, tile_dst)), tile_count)

    def finish(packed, part, hot, pick, edges):
        mine = lax.all_to_all(
            part.reshape(n_row * n_col, *part.shape[2:]), ("row", "col"), 0, 0
        ).reshape(part.shape)
        other = lax.ppermute(mine, "rep", swap)
        return pl.pallas_call(
            functools.partial(second_kernel, sizes, packed),
            out_shape=(shape((n_col, height, size), BF16), shape((height, size), BF16)),
            in_specs=[vmem] * 5,
            out_specs=(vmem,) * 2,
            scratch_shapes=[pltpu.VMEM((slots, height, size), BF16), best],
            compiler_params=limit,
            name="round_two" if packed else "round_two_all",
        )(mine, other, hot, pick, edges)

    def common(part, hot, pick, edges):
        return finish(True, part, hot, pick, edges)

    def crowded(part, hot, pick, edges):
        full = pl.pallas_call(
            first_kernel_all,
            out_shape=shape((n_row, n_col, height, size), BF16),
            in_specs=[vmem] * 2,
            out_specs=vmem,
            scratch_shapes=[best],
            compiler_params=limit,
            name="round_one_all",
        )(hot, edges)
        return finish(False, full, hot, pick, edges)

    part, own = lax.cond(over[0] > 0, crowded, common, part, hot, pick, edges)
    fresh = lax.all_to_all(part, "col", 0, 0)
    distances, sums = pl.pallas_call(
        final_kernel,
        out_shape=(pltpu.VMEM((height, size), F32), shape((1, height), F32)),
        in_specs=[vmem, vmem],
        out_specs=(vmem, vmem),
        compiler_params=limit,
        name="decode",
    )(fresh, own)
    return distances, sums + lax.ppermute(sums, "rep", swap)


def solution(mesh):
    cut = ("row", "col", "rep")
    return jax.shard_map(
        per_device,
        mesh=mesh,
        in_specs=(P(), P(cut, None, None), P(cut), P(cut), P(cut)),
        out_specs=(P(None, cut), P(("row", "col"), None)),
        check_vma=False,
    )
```

time: 34.9 us -> 31.7 us (0.908)
  blocking collectives: 26.8 us -> 24 us
  waiting for transfers between devices: 2.69 us -> 1.88 us
  local copies, waits for them, and re-layouts: 0 us -> 0.62 us
    all_to_all x1, blocking collectives: 18.7 us -> 15.8 us  [finish(): lax.all_to_all(part.reshape(n_row * n_col, *part.shape[2:]), ('row', 'col...]
    ppermute x2, waiting for transfers between devices: 2.69 us -> 1.88 us  [the longest x1 1.35 us: finish(): other = lax.ppermute(mine, 'rep', swap)]
    unnamed x0 -> x1, local copies, waits for them, and re-layouts: none -> 0.62 us
  transfers between devices with their start and end apart: 2 -> 2, of which waited for: 2 -> 2; matrix products, arithmetic and copies ran while one was open for 0% -> 2% of each run, Pallas kernels for 0% -> 0%
where the time goes in v3:
time: 31.7 us; the launch traced here: 31.5 us
  blocking collectives  24 us (76%)
  Pallas kernels  3.16 us (10%)
  waiting for transfers between devices  1.88 us (6%)
  between operations  1.31 us (4%)
  local copies, waits for them, and re-layouts  0.62 us (2%)
  other arithmetic  0.51 us (2%)
    all_to_all x1, blocking collectives, finish(): lax.all_to_all(part.reshape(n_row * n_col, *part.shape[2:]), ('row', 'col...  15.8 us
    all_to_all x1, blocking collectives, per_device(): fresh = lax.all_to_all(part, 'col', 0, 0)  8.11 us
    pallas_call x1, Pallas kernels, per_device(): pl.pallas_call(functools.partial(first_kernel, sizes), out_shape=(shape((...  2.48 us
    ppermute x1, waiting for transfers between devices, finish(): other = lax.ppermute(mine, 'rep', swap)  1.35 us
  transfers between devices with their start and end apart: 2, of which 2 were waited for; matrix products, arithmetic and copies ran while one was open for 2% of the time, Pallas kernels for 0%

profile of v3, /device:TPU:0, one launch (start us, length us, event | category | flops | bytes accessed | tf_op | source)
XLA Modules:
  0.0 31.5 jit_solution(5833234576049224950)
XLA Ops:
  1.3 2.5 %round_one.1 = (bf16[8,4,128,128]{3,2,1,0:T(8,128)(2,1)S(1)}, bf16[8,64,128]{2,1,0:T(8,128)(2,1)S(1)}, bf16[64,128]{1,0:T(8,128)(2,1)S(1)}, bf16[4,4,32,128]{3,2,1,0:T(8,128)(2,1)S(1)}, s32[1]{0:T(128)S(4)}) custom-call(s32[1,64]{1,0:T(1,128)} %bitcast.12, s32[32,128,128]{2,1,0:T(8,128)} %weights.1, s32[32]{0:T(128)} %src.1, s32[32]{0:T(128)} %dst.1, ...), custom_call_target="tpu_custom_call" | custom-call | tf_op jit(solution)/shard_map/round_one/pallas_call | solution.py:153
  3.8 17.8 %conditional.1 = ((bf16[4,64,128]{2,1,0:T(8,128)(2,1)S(1)}, bf16[64,128]{1,0:T(8,128)(2,1)S(1)})) conditional(s32[]{:T(128)} %bitcast.5, (bf16[4,4,32,128]{3,2,1,0:T(8,128)(2,1)S(1)}, bf16[8,64,128]{2,1,0:T(8,128)(2,1)S(1)}, bf16[64,128]{1,0:T(8,128)(2,1)S(1)}, bf16[8,4,128,128]{3,2,1,0:T(8,128)(2,1)S(1)}) %tuple.14, ...), branch_computations={%region_0.0_spmd, %region_1.0_spmd} | conditional | bytes 1572912 | solution.py:208
  3.8 15.8 %all_to_all.13 = bf16[16,32,128]{2,1,0:T(8,128)(2,1)S(1)} all-to-all(bf16[16,32,128]{2,1,0:T(8,128)(2,1)S(1)} %bitcast.11), channel_id=1, replica_groups=mesh['row'=4,'col'=4,'rep'=2] {'row','col'}, dimensions={0} | all-to-all | bytes 262144 | tf_op jit(solution)/shard_map/cond/branch_0_fun/all_to_all | solution.py:179
  19.6 0.0 collective-permute-start
  19.6 1.3 %collective-permute-done.other = bf16[4,4,32,128]{3,2,1,0:T(8,128)(2,1)S(1)} collective-permute-done((bf16[4,4,32,128]{3,2,1,0:T(8,128)(2,1)S(1)}, bf16[4,4,32,128]{3,2,1,0:T(8,128)(2,1)S(1)}, u32[]{:S(2)}, u32[]{:S(2)}) %collective-permute-start) | collective-permute-done | bytes 131104 | tf_op jit(solution)/shard_map/cond/branch_0_fun/ppermute | solution.py:182
  21.0 0.6 %round_two.1 = (bf16[4,64,128]{2,1,0:T(8,128)(2,1)S(1)}, bf16[64,128]{1,0:T(8,128)(2,1)S(1)}) custom-call(bf16[4,4,32,128]{3,2,1,0:T(8,128)(2,1)S(1)} %bitcast.10, bf16[4,4,32,128]{3,2,1,0:T(8,128)(2,1)S(1)} %collective-permute-done.other, bf16[8,64,128]{2,1,0:T(8,128)(2,1)S(1)} %get-tuple-element.15.hot, bf16[64,128]{1,0:T(8,128)(2,1)S(1)} %get-tuple-element.16.pick, ...), custom_call_target="tpu_custom_call" | custom-call | tf_op jit(solution)/shard_map/cond/branch_0_fun/round_two/pallas_call | solution.py:183
  21.5 8.1 %all_to_all.15.fresh = bf16[4,64,128]{2,1,0:T(8,128)(2,1)S(1)} all-to-all(bf16[4,64,128]{2,1,0:T(8,128)(2,1)S(1)} %get-tuple-element.37), channel_id=1, replica_groups=mesh['row'=4,'col'=4,'rep'=2] {'col'}, dimensions={0} | all-to-all | bytes 131072 | tf_op jit(solution)/shard_map/all_to_all | solution.py:209
  29.7 0.1 decode.1
  29.8 0.1 collective-permute-start.2
  29.9 0.6 %copy.11 = f32[64,128]{1,0:T(8,128)} copy(f32[64,128]{1,0:T(8,128)S(1)} %get-tuple-element.45) | data formatting | bytes 65536
  30.5 0.5 %collective-permute-done.2 = f32[1,64]{1,0:T(1,128)S(1)} collective-permute-done((f32[1,64]{1,0:T(1,128)S(1)}, f32[1,64]{1,0:T(1,128)S(1)}, u32[]{:S(2)}, u32[]{:S(2)}) %collective-permute-start.2) | collective-permute-done | bytes 288 | tf_op jit(solution)/shard_map/ppermute | solution.py:218
  31.0 0.5 %add.3 = f32[1,64]{1,0:T(1,128)} add(f32[1,64]{1,0:T(1,128)S(1)} %get-tuple-element.40, f32[1,64]{1,0:T(1,128)S(1)} %collective-permute-done.2) | non-fusion elementwise | flops 64 | bytes 768 | tf_op jit(solution)/shard_map/add | solution.py:218
Async XLA Ops:
  19.6 1.3 %collective-permute-start = (bf16[4,4,32,128]{3,2,1,0:T(8,128)(2,1)S(1)}, bf16[4,4,32,128]{3,2,1,0:T(8,128)(2,1)S(1)}, u32[]{:S(2)}, u32[]{:S(2)}) collective-permute-start(bf16[4,4,32,128]{3,2,1,0:T(8,128)(2,1)S(1)} %bitcast.9), channel_id=1, source_target_pairs={{0,1},{1,0},{2,3},{3,2},{4,5},{5,4},{6,7},{7,6},{8,9},{9,8},{10,11... | collective-permute-start | bytes 393224 | tf_op jit(solution)/shard_map/cond/branch_0_fun/ppermute | solution.py:182
  29.8 1.2 %collective-permute-start.2 = (f32[1,64]{1,0:T(1,128)S(1)}, f32[1,64]{1,0:T(1,128)S(1)}, u32[]{:S(2)}, u32[]{:S(2)}) collective-permute-start(f32[1,64]{1,0:T(1,128)S(1)} %get-tuple-element.40), channel_id=1, source_target_pairs={{0,1},{1,0},{2,3},{3,2},{4,5},{5,4},{6,7},{7,6},{8,9},{9,8},{10,11... | collective-permute-start | bytes 776 | tf_op jit(solution)/shard_map/ppermute | solution.py:218

commit v4 on v3

--- a/solution.py
+++ b/solution.py
@@ -9,34 +9,36 @@
 
 BLK_DEV = 1
 STEP = 7.5
-HALF = 63.0
+TOP = 126.0
 FAR = 255.0
-CHUNKS = 8
+CHUNKS = 4
 F32, BF16 = jnp.float32, jnp.bfloat16
 
 
-def relax(dist, edges, best):
-    for q in range(dist.shape[0]):
-        left = dist[q]
-        for d in range(best.shape[0]):
-            total = jnp.dot(left, edges[q, d], preferred_element_type=F32)
-            best[d] = total if q == 0 else jnp.maximum(best[d], total)
+def relax(dist, code, q_of, d_of, best, tiles):
+    for k in tiles:
+        total = jnp.dot(dist[q_of[k]], code[k], preferred_element_type=F32)
+        d = d_of[k]
+        best[d] = jnp.maximum(best[d], total)
+
+
+def log(n):
+    return n.bit_length() - 1
 
 
 def column_of(vertex, size, n_col, n_rep):
-    shift = (size * BLK_DEV * n_rep).bit_length() - 1
-    return lax.shift_right_logical(vertex, shift) & (n_col - 1)
+    return lax.shift_right_logical(vertex, log(size * n_rep)) & (n_col - 1)
 
 
 def spread(part, best):
-    coded = (best[...] * 2.0**-HALF).astype(BF16)
+    coded = best[: part.shape[1]].astype(BF16)
     for r in range(part.shape[0]):
         part[r] = coded
 
 
 def first_kernel(
     sizes, sources, weights, src, dst, count,
-    edges, hot, pick, part, over,
+    code, hot, pick, part, over, q_of, d_of,
     few, best, raw, ids, s_src, s_dst, sems, small,
 ):
     n_row, n_col, n_rep = sizes
@@ -57,7 +59,7 @@
     ]
     for copy in copies:
         copy.start()
-    edges[...] = jnp.zeros_like(edges)
+    best[...] = jnp.zeros_like(best)
     for copy in firsts:
         copy.wait()
     me = lax.axis_index("col")
@@ -80,29 +82,30 @@
     vertex = jnp.sum(jnp.where(taken, along[:room].astype(F32) + 1.0, 0.0), axis=1, keepdims=True) - 1.0
     for q in range(n_row * n_rep):
         at = lane + (((q // n_rep) * n_col + me) * n_rep + q % n_rep) * size
-        hot[q] = jnp.where(down == at, 2.0**HALF, 0.0).astype(BF16)
-        few[q] = jnp.where(vertex == at[:room].astype(F32), 2.0**HALF, 0.0).astype(BF16)
+        hot[q] = jnp.where(down == at, 2.0**TOP, 0.0).astype(BF16)
+        few[q] = jnp.where(vertex == at[:room].astype(F32), 2.0**TOP, 0.0).astype(BF16)
     live = count[0]
+    for k in range(tiles):
+        q_of[k] = lax.shift_right_logical(s_src[k], log(n_col * n_rep)) * n_rep + (s_src[k] & (n_rep - 1))
+        d = lax.shift_right_logical(s_dst[k], log(n_rep)) & (n_col - 1)
+        d_of[k] = jnp.where(k < live, d, n_col)
     for c, copy in enumerate(copies):
         copy.wait()
-        for k in range(c * step, (c + 1) * step):
+        mine = range(c * step, (c + 1) * step)
+        for k in mine:
             w = raw[k].astype(F32).astype(BF16)
-            bound = jnp.where(k < live, 0.5, 1e9).astype(BF16)
-            coded = jnp.where(w > bound, jnp.exp2(BF16(HALF) - BF16(STEP) * w), BF16(0.0))
-            piece = s_src[k] // BLK_DEV
-            q = piece // (n_col * n_rep) * n_rep + lax.rem(piece, n_rep)
-            d = lax.rem(s_dst[k] // BLK_DEV // n_rep, n_col)
-            edges[q, d] = jnp.maximum(edges[q, d], coded)
-    relax(few, edges, best)
+            code[k] = jnp.where(w > 0, jnp.exp2(BF16(-STEP) * w), BF16(0.0))
+    relax(few, code, q_of, d_of, best, range(tiles))
     spread(part, best)
 
 
-def first_kernel_all(hot, edges, part, best):
-    relax(hot, edges, best)
+def first_kernel_all(hot, code, q_of, d_of, part, best):
+    best[...] = jnp.zeros_like(best)
+    relax(hot, code, q_of, d_of, best, range(code.shape[0]))
     spread(part, best)
 
 
-def second_kernel(sizes, packed, mine, other, hot, pick, edges, part, own, dist, best):
+def second_kernel(sizes, packed, mine, other, hot, pick, code, q_of, d_of, part, own, dist, best):
     n_row, n_col, n_rep = sizes
     rep = lax.axis_index("rep")
     for r in range(n_row):
@@ -118,14 +121,15 @@
             q = r * n_rep + p
             dist[q] = jnp.maximum(jnp.where(rep == p, got[0], got[1]), hot[q])
     own[...] = dist[lax.axis_index("row") * n_rep + rep]
-    relax(dist, edges, best)
-    part[...] = best[...].astype(BF16)
+    best[...] = jnp.zeros_like(best)
+    relax(dist, code, q_of, d_of, best, range(code.shape[0]))
+    part[...] = best[:n_col].astype(BF16)
 
 
 def final_kernel(fresh, own, distances, sums):
     best = jnp.max(fresh[...].astype(F32), axis=0)
-    best = jnp.maximum(best, own[...].astype(F32) * 2.0**HALF)
-    level = jnp.ceil((2 * HALF - 0.22 - jnp.log2(jnp.maximum(best, 2.0**-125))) / STEP)
+    best = jnp.maximum(best, own[...].astype(F32))
+    level = jnp.ceil((TOP - 0.22 - jnp.log2(jnp.maximum(best, 2.0**-125))) / STEP)
     value = jnp.where(best > 0.0, level, FAR)
     distances[...] = jnp.where(value > 0.0, value, 0.0)
     inverse = jnp.where(value > 0.0, 1.0 / jnp.maximum(value, 1.0), 0.0)
@@ -149,21 +153,23 @@
     limit = pltpu.CompilerParams(vmem_limit_bytes=14 << 20)
     shape = jax.ShapeDtypeStruct
     swap = [(i, (i + 1) % n_rep) for i in range(n_rep)]
-    best = pltpu.VMEM((n_col, height, size), F32)
-    edges, hot, pick, part, over = pl.pallas_call(
+    best = pltpu.VMEM((n_col + 1, height, size), F32)
+    code, hot, pick, part, over, *places = pl.pallas_call(
         functools.partial(first_kernel, sizes),
         out_shape=(
-            shape((slots, n_col, size, size), BF16),
+            shape((tiles, size, size), BF16),
             shape((slots, height, size), BF16),
             shape((height, n_col * room), BF16),
             shape((n_row, n_col, room, size), BF16),
             pltpu.SMEM((1,), jnp.int32),
+            pltpu.SMEM((tiles,), jnp.int32),
+            pltpu.SMEM((tiles,), jnp.int32),
         ),
         in_specs=[hbm] * 4 + [smem],
-        out_specs=(vmem,) * 4 + (smem,),
+        out_specs=(vmem,) * 4 + (smem,) * 3,
         scratch_shapes=[
             pltpu.VMEM((slots, room, size), BF16),
-            pltpu.VMEM((n_col, room, size), F32),
+            pltpu.VMEM((n_col + 1, room, size), F32),
             pltpu.VMEM((tiles, size, size), jnp.int32),
             pltpu.VMEM((1, height), jnp.int32),
             pltpu.SMEM((tiles,), jnp.int32),
@@ -175,7 +181,7 @@
         name="round_one",
     )(*map(in_hbm, (sources.reshape(1, height), tile_weights, tile_src, tile_dst)), tile_count)
 
-    def finish(packed, part, hot, pick, edges):
+    def finish(packed, part, hot, pick, code, *places):
         mine = lax.all_to_all(
             part.reshape(n_row * n_col, *part.shape[2:]), ("row", "col"), 0, 0
         ).reshape(part.shape)
@@ -183,29 +189,29 @@
         return pl.pallas_call(
             functools.partial(second_kernel, sizes, packed),
             out_shape=(shape((n_col, height, size), BF16), shape((height, size), BF16)),
-            in_specs=[vmem] * 5,
+            in_specs=[vmem] * 5 + [smem] * 2,
             out_specs=(vmem,) * 2,
             scratch_shapes=[pltpu.VMEM((slots, height, size), BF16), best],
             compiler_params=limit,
             name="round_two" if packed else "round_two_all",
-        )(mine, other, hot, pick, edges)
-
-    def common(part, hot, pick, edges):
-        return finish(True, part, hot, pick, edges)
-
-    def crowded(part, hot, pick, edges):
+        )(mine, other, hot, pick, code, *places)
+
+    def common(part, hot, pick, code, *places):
+        return finish(True, part, hot, pick, code, *places)
+
+    def crowded(part, hot, pick, code, *places):
         full = pl.pallas_call(
             first_kernel_all,
             out_shape=shape((n_row, n_col, height, size), BF16),
-            in_specs=[vmem] * 2,
+            in_specs=[vmem] * 2 + [smem] * 2,
             out_specs=vmem,
             scratch_shapes=[best],
             compiler_params=limit,
             name="round_one_all",
-        )(hot, edges)
-        return finish(False, full, hot, pick, edges)
-
-    part, own = lax.cond(over[0] > 0, crowded, common, part, hot, pick, edges)
+        )(hot, code, *places)
+        return finish(False, full, hot, pick, code, *places)
+
+    part, own = lax.cond(over[0] > 0, crowded, common, part, hot, pick, code, *places)
     fresh = lax.all_to_all(part, "col", 0, 0)
     distances, sums = pl.pallas_call(
         final_kernel,

time: 31.7 us -> 31.4 us (level)
  Pallas kernels: 3.16 us -> 2.77 us
    pallas_call x1, Pallas kernels: 2.48 us -> 2.02 us  [per_device(): pl.pallas_call(functools.partial(first_kernel, sizes), out_shape=(shape((...]
where the time goes in v4:
time: 31.4 us; the launch traced here: 31.1 us
  blocking collectives  23.9 us (76%)
  Pallas kernels  2.77 us (9%)
  waiting for transfers between devices  1.88 us (6%)
  between operations  1.31 us (4%)
  local copies, waits for them, and re-layouts  0.62 us (2%)
  other arithmetic  0.51 us (2%)
    all_to_all x1, blocking collectives, finish(): lax.all_to_all(part.reshape(n_row * n_col, *part.shape[2:]), ('row', 'col...  15.8 us
    all_to_all x1, blocking collectives, per_device(): fresh = lax.all_to_all(part, 'col', 0, 0)  8.11 us
    pallas_call x1, Pallas kernels, per_device(): pl.pallas_call(functools.partial(first_kernel, sizes), out_shape=(shape((...  2.02 us
    ppermute x1, waiting for transfers between devices, finish(): other = lax.ppermute(mine, 'rep', swap)  1.35 us
    pallas_call x1, Pallas kernels, finish(): pl.pallas_call(functools.partial(second_kernel, sizes, packed), out_shape...  0.63 us
  transfers between devices with their start and end apart: 2, of which 2 were waited for; matrix products, arithmetic and copies ran while one was open for 2% of the time, Pallas kernels for 0%

profile of v4, /device:TPU:0, one launch (start us, length us, event | category | flops | bytes accessed | tf_op | source)
XLA Modules:
  0.0 31.1 jit_solution(4117857242376266587)
XLA Ops:
  1.3 2.0 %round_one.1 = (bf16[32,128,128]{2,1,0:T(8,128)(2,1)S(1)}, bf16[8,64,128]{2,1,0:T(8,128)(2,1)S(1)}, bf16[64,128]{1,0:T(8,128)(2,1)S(1)}, bf16[4,4,32,128]{3,2,1,...) custom-call(s32[1,64]{1,0:T(1,128)} %bitcast.12, s32[32,128,128]{2,1,0:T(8,128)} %weights.1, ...), custom_call_target="tpu_custom_call" | custom-call | tf_op jit(solution)/shard_map/round_one/pallas_call | solution.py:157
  3.3 17.8 %conditional.1 = ((bf16[4,64,128]{2,1,0:T(8,128)(2,1)S(1)}, bf16[64,128]{1,0:T(8,128)(2,1)S(1)})) conditional(s32[]{:T(128)} %bitcast.5, (bf16[4,4,32,128]{3,2,1,0:T(8,128)(2,1)S(1)}, bf16[8,64,128]{2,1,0:T(8,128)(2,1)S(1)}, bf16[64,128]{1,0:T(8,128)(2,1)S(1)}, bf16[32,128,128]{2,1,0:T(8,128)(2,1)S(1)}, s32[32]{0:T(128)S(4)}, ...), branch_computations={%region_0.0_spmd, %region_1.0_spmd} | conditional | bytes 1572912 | solution.py:214
  3.3 15.8 %all_to_all.13 = bf16[16,32,128]{2,1,0:T(8,128)(2,1)S(1)} all-to-all(bf16[16,32,128]{2,1,0:T(8,128)(2,1)S(1)} %bitcast.11), channel_id=1, replica_groups=mesh['row'=4,'col'=4,'rep'=2] {'row','col'}, dimensions={0} | all-to-all | bytes 262144 | tf_op jit(solution)/shard_map/cond/branch_0_fun/all_to_all | solution.py:185
  19.2 0.0 collective-permute-start
  19.2 1.3 %collective-permute-done.other = bf16[4,4,32,128]{3,2,1,0:T(8,128)(2,1)S(1)} collective-permute-done((bf16[4,4,32,128]{3,2,1,0:T(8,128)(2,1)S(1)}, bf16[4,4,32,128]{3,2,1,0:T(8,128)(2,1)S(1)}, u32[]{:S(2)}, u32[]{:S(2)}) %collective-permute-start) | collective-permute-done | bytes 131104 | tf_op jit(solution)/shard_map/cond/branch_0_fun/ppermute | solution.py:188
  20.5 0.6 %round_two.1 = (bf16[4,64,128]{2,1,0:T(8,128)(2,1)S(1)}, bf16[64,128]{1,0:T(8,128)(2,1)S(1)}) custom-call(bf16[4,4,32,128]{3,2,1,0:T(8,128)(2,1)S(1)} %bitcast.10, bf16[4,4,32,128]{3,2,1,0:T(8,128)(2,1)S(1)} %collective-permute-done.other, bf16[8,64,128]{2,1,0:T(8,128)(2,1)S(1)} %get-tuple-element.23.hot, bf16[64,128]{1,0:T(8,128)(2,1)S(1)} %get-tuple-element.24.pick, ...), custom_call_target="tpu_custom_call" | custom-call | tf_op jit(solution)/shard_map/cond/branch_0_fun/round_two/pallas_call | solution.py:189
  21.1 8.1 %all_to_all.15.fresh = bf16[4,64,128]{2,1,0:T(8,128)(2,1)S(1)} all-to-all(bf16[4,64,128]{2,1,0:T(8,128)(2,1)S(1)} %get-tuple-element.53), channel_id=1, replica_groups=mesh['row'=4,'col'=4,'rep'=2] {'col'}, dimensions={0} | all-to-all | bytes 131072 | tf_op jit(solution)/shard_map/all_to_all | solution.py:215
  29.3 0.1 decode.1
  29.4 0.1 collective-permute-start.2
  29.5 0.6 %copy.11 = f32[64,128]{1,0:T(8,128)} copy(f32[64,128]{1,0:T(8,128)S(1)} %get-tuple-element.61) | data formatting | bytes 65536
  30.1 0.5 %collective-permute-done.2 = f32[1,64]{1,0:T(1,128)S(1)} collective-permute-done((f32[1,64]{1,0:T(1,128)S(1)}, f32[1,64]{1,0:T(1,128)S(1)}, u32[]{:S(2)}, u32[]{:S(2)}) %collective-permute-start.2) | collective-permute-done | bytes 288 | tf_op jit(solution)/shard_map/ppermute | solution.py:224
  30.6 0.5 %add.3 = f32[1,64]{1,0:T(1,128)} add(f32[1,64]{1,0:T(1,128)S(1)} %get-tuple-element.56, f32[1,64]{1,0:T(1,128)S(1)} %collective-permute-done.2) | non-fusion elementwise | flops 64 | bytes 768 | tf_op jit(solution)/shard_map/add | solution.py:224
Async XLA Ops:
  19.2 1.3 %collective-permute-start = (bf16[4,4,32,128]{3,2,1,0:T(8,128)(2,1)S(1)}, bf16[4,4,32,128]{3,2,1,0:T(8,128)(2,1)S(1)}, u32[]{:S(2)}, u32[]{:S(2)}) collective-permute-start(bf16[4,4,32,128]{3,2,1,0:T(8,128)(2,1)S(1)} %bitcast.9), channel_id=1, source_target_pairs={{0,1},{1,0},{2,3},{3,2},{4,5},{5,4},{6,7},{7,6},{8,9},{9,8},{10,11... | collective-permute-start | bytes 393224 | tf_op jit(solution)/shard_map/cond/branch_0_fun/ppermute | solution.py:188
  29.4 1.2 %collective-permute-start.2 = (f32[1,64]{1,0:T(1,128)S(1)}, f32[1,64]{1,0:T(1,128)S(1)}, u32[]{:S(2)}, u32[]{:S(2)}) collective-permute-start(f32[1,64]{1,0:T(1,128)S(1)} %get-tuple-element.56), channel_id=1, source_target_pairs={{0,1},{1,0},{2,3},{3,2},{4,5},{5,4},{6,7},{7,6},{8,9},{9,8},{10,11... | collective-permute-start | bytes 776 | tf_op jit(solution)/shard_map/ppermute | solution.py:224

commit v5 on v3

--- a/solution.py
+++ b/solution.py
@@ -9,27 +9,30 @@
 
 BLK_DEV = 1
 STEP = 7.5
-HALF = 63.0
+TOP = 126.0
 FAR = 255.0
-CHUNKS = 8
+CHUNKS = 4
 F32, BF16 = jnp.float32, jnp.bfloat16
 
 
 def relax(dist, edges, best):
-    for q in range(dist.shape[0]):
-        left = dist[q]
-        for d in range(best.shape[0]):
-            total = jnp.dot(left, edges[q, d], preferred_element_type=F32)
-            best[d] = total if q == 0 else jnp.maximum(best[d], total)
+    width = best.shape[0]
+    for q, left in enumerate(dist):
+        for d in range(width):
+            total = jnp.dot(left, edges[q * width + d], preferred_element_type=F32)
+            best[d] = jnp.maximum(best[d], total) if q else total
+
+
+def log(n):
+    return n.bit_length() - 1
 
 
 def column_of(vertex, size, n_col, n_rep):
-    shift = (size * BLK_DEV * n_rep).bit_length() - 1
-    return lax.shift_right_logical(vertex, shift) & (n_col - 1)
+    return lax.shift_right_logical(vertex, log(size * n_rep)) & (n_col - 1)
 
 
 def spread(part, best):
-    coded = (best[...] * 2.0**-HALF).astype(BF16)
+    coded = best[...].astype(BF16)
     for r in range(part.shape[0]):
         part[r] = coded
 
@@ -78,57 +81,69 @@
     order = lax.broadcasted_iota(jnp.int32, (room, height), 0).astype(F32)
     taken = (order == rank_along) & (col_along[:room] == me)
     vertex = jnp.sum(jnp.where(taken, along[:room].astype(F32) + 1.0, 0.0), axis=1, keepdims=True) - 1.0
+    rep = lax.axis_index("rep")
     for q in range(n_row * n_rep):
-        at = lane + (((q // n_rep) * n_col + me) * n_rep + q % n_rep) * size
-        hot[q] = jnp.where(down == at, 2.0**HALF, 0.0).astype(BF16)
-        few[q] = jnp.where(vertex == at[:room].astype(F32), 2.0**HALF, 0.0).astype(BF16)
+        at = lane + ((q % n_row * n_col + me) * n_rep + (rep ^ (q // n_row))) * size
+        hot[q] = jnp.where(down == at, 2.0**TOP, 0.0).astype(BF16)
+        few[q] = jnp.where(vertex == at[:room].astype(F32), 2.0**TOP, 0.0).astype(BF16)
     live = count[0]
     for c, copy in enumerate(copies):
         copy.wait()
         for k in range(c * step, (c + 1) * step):
+            q = ((s_src[k] & 1) ^ rep) * n_row + lax.shift_right_logical(s_src[k], log(n_col * n_rep))
+            d = lax.shift_right_logical(s_dst[k], log(n_rep)) & (n_col - 1)
+            at = jnp.where(k < live, q * n_col + d, n_row * n_rep * n_col)
             w = raw[k].astype(F32).astype(BF16)
-            bound = jnp.where(k < live, 0.5, 1e9).astype(BF16)
-            coded = jnp.where(w > bound, jnp.exp2(BF16(HALF) - BF16(STEP) * w), BF16(0.0))
-            piece = s_src[k] // BLK_DEV
-            q = piece // (n_col * n_rep) * n_rep + lax.rem(piece, n_rep)
-            d = lax.rem(s_dst[k] // BLK_DEV // n_rep, n_col)
-            edges[q, d] = jnp.maximum(edges[q, d], coded)
-    relax(few, edges, best)
+            coded = jnp.where(w > 0, jnp.exp2(BF16(-STEP) * w), BF16(0.0))
+            edges[at] = jnp.maximum(edges[at], coded)
+    relax([few[q] for q in range(n_row * n_rep)], edges, best)
     spread(part, best)
 
 
 def first_kernel_all(hot, edges, part, best):
-    relax(hot, edges, best)
+    relax([hot[q] for q in range(hot.shape[0])], edges, best)
     spread(part, best)
 
 
-def second_kernel(sizes, packed, mine, other, hot, pick, edges, part, own, dist, best):
+def second_kernel(sizes, packed, got, hot, pick, edges, theirs, part, own, best):
     n_row, n_col, n_rep = sizes
-    rep = lax.axis_index("rep")
+    dist = []
     for r in range(n_row):
-        got = []
-        for side in (mine, other):
-            rows = side[r]
-            if packed:
-                rows = rows.reshape(-1, rows.shape[-1])
-                got.append(jnp.dot(pick[...], rows, preferred_element_type=F32).astype(BF16))
-            else:
-                got.append(jnp.max(rows, axis=0))
-        for p in range(n_rep):
-            q = r * n_rep + p
-            dist[q] = jnp.maximum(jnp.where(rep == p, got[0], got[1]), hot[q])
-    own[...] = dist[lax.axis_index("row") * n_rep + rep]
+        if packed:
+            rows = got[r].reshape(-1, got.shape[-1])
+            value = jnp.dot(pick[...], rows, preferred_element_type=F32).astype(BF16)
+        else:
+            value = jnp.max(got[r], axis=0)
+        dist.append(jnp.maximum(value, hot[r]))
+    here = lax.axis_index("row")
+    value = dist[0]
+    for r in range(1, n_row):
+        value = jnp.where(here == r, dist[r], value)
+    own[...] = value
     relax(dist, edges, best)
-    part[...] = best[...].astype(BF16)
-
-
-def final_kernel(fresh, own, distances, sums):
-    best = jnp.max(fresh[...].astype(F32), axis=0)
-    best = jnp.maximum(best, own[...].astype(F32) * 2.0**HALF)
-    level = jnp.ceil((2 * HALF - 0.22 - jnp.log2(jnp.maximum(best, 2.0**-125))) / STEP)
-    value = jnp.where(best > 0.0, level, FAR)
-    distances[...] = jnp.where(value > 0.0, value, 0.0)
+    part[:, 0] = best[...].astype(BF16)
+    relax(dist, theirs.at[pl.ds(n_row * n_col, n_row * n_col)], best)
+    part[:, 1] = best[...].astype(BF16)
+
+
+def merge_kernel(fresh, own, merged):
+    merged[0] = jnp.maximum(jnp.max(fresh[:, 0], axis=0), own[...])
+    merged[1] = jnp.max(fresh[:, 1], axis=0)
+
+
+def decode(code):
+    code = code.astype(F32)
+    level = jnp.ceil((TOP - 0.22 - jnp.log2(jnp.maximum(code, 2.0**-125))) / STEP)
+    value = jnp.where(code > 0.0, level, FAR)
+    return jnp.where(value > 0.0, value, 0.0)
+
+
+def final_kernel(mine, theirs, distances, sums):
+    value = decode(jnp.maximum(mine[0], theirs[1]))
+    other = decode(jnp.maximum(mine[1], theirs[0]))
+    distances[...] = value
     inverse = jnp.where(value > 0.0, 1.0 / jnp.maximum(value, 1.0), 0.0)
+    inverse += jnp.where(other > 0.0, 1.0 / jnp.maximum(other, 1.0), 0.0)
     sums[...] = jnp.sum(inverse.T, axis=0, keepdims=True)
 
 
@@ -146,14 +161,15 @@
     vmem = pl.BlockSpec(memory_space=pltpu.VMEM)
     smem = pl.BlockSpec(memory_space=pltpu.SMEM)
     hbm = pl.BlockSpec(memory_space=pltpu.HBM)
-    limit = pltpu.CompilerParams(vmem_limit_bytes=14 << 20)
+    limit = pltpu.CompilerParams(vmem_limit_bytes=28 << 20)
     shape = jax.ShapeDtypeStruct
     swap = [(i, (i + 1) % n_rep) for i in range(n_rep)]
+    places = slots * n_col + 1
     best = pltpu.VMEM((n_col, height, size), F32)
     edges, hot, pick, part, over = pl.pallas_call(
         functools.partial(first_kernel, sizes),
         out_shape=(
-            shape((slots, n_col, size, size), BF16),
+            shape((places, size, size), BF16),
             shape((slots, height, size), BF16),
             shape((height, n_col * room), BF16),
             shape((n_row, n_col, room, size), BF16),
@@ -176,19 +192,19 @@
     )(*map(in_hbm, (sources.reshape(1, height), tile_weights, tile_src, tile_dst)), tile_count)
 
     def finish(packed, part, hot, pick, edges):
-        mine = lax.all_to_all(
+        theirs = lax.ppermute(edges, "rep", swap)
+        got = lax.all_to_all(
             part.reshape(n_row * n_col, *part.shape[2:]), ("row", "col"), 0, 0
         ).reshape(part.shape)
-        other = lax.ppermute(mine, "rep", swap)
         return pl.pallas_call(
             functools.partial(second_kernel, sizes, packed),
-            out_shape=(shape((n_col, height, size), BF16), shape((height, size), BF16)),
+            out_shape=(shape((n_col, n_rep, height, size), BF16), shape((height, size), BF16)),
             in_specs=[vmem] * 5,
             out_specs=(vmem,) * 2,
-            scratch_shapes=[pltpu.VMEM((slots, height, size), BF16), best],
+            scratch_shapes=[best],
             compiler_params=limit,
             name="round_two" if packed else "round_two_all",
-        )(mine, other, hot, pick, edges)
+        )(got, hot, pick, edges, theirs)
 
     def common(part, hot, pick, edges):
         return finish(True, part, hot, pick, edges)
@@ -207,15 +223,23 @@
 
     part, own = lax.cond(over[0] > 0, crowded, common, part, hot, pick, edges)
     fresh = lax.all_to_all(part, "col", 0, 0)
-    distances, sums = pl.pallas_call(
+    mine = pl.pallas_call(
+        merge_kernel,
+        out_shape=shape((n_rep, height, size), BF16),
+        in_specs=[vmem] * 2,
+        out_specs=vmem,
+        compiler_params=limit,
+        name="merge",
+    )(fresh, own)
+    theirs = lax.ppermute(mine, "rep", swap)
+    return pl.pallas_call(
         final_kernel,
-        out_shape=(pltpu.VMEM((height, size), F32), shape((1, height), F32)),
-        in_specs=[vmem, vmem],
-        out_specs=(vmem, vmem),
+        out_shape=(shape((height, size), F32), shape((1, height), F32)),
+        in_specs=[vmem] * 2,
+        out_specs=(vmem,) * 2,
         compiler_params=limit,
         name="decode",
-    )(fresh, own)
-    return distances, sums + lax.ppermute(sums, "rep", swap)
+    )(mine, theirs)
 
 
 def solution(mesh):

time: 31.7 us -> 31 us (0.978)
  waiting for transfers between devices: 1.88 us -> 1.2 us
  local copies, waits for them, and re-layouts: 0.62 us -> 0 us
  starting transfers between devices: 0.07 us -> 0.63 us
  other arithmetic: 0.51 us -> 0 us
    ppermute x2, waiting for transfers between devices: 1.88 us -> 1.2 us  [the longest x1 1.19 us: per_device(): theirs = lax.ppermute(mine, 'rep', swap)]
    unnamed x1 -> x0, local copies, waits for them, and re-layouts: 0.62 us -> none
    pallas_call x1 -> x2, Pallas kernels: 0.13 us -> 0.68 us  [the longest x1 0.65 us: per_device(): pl.pallas_call(final_kernel, out_shape=(shape((height, size), F32), shape...]
    ppermute x2, starting transfers between devices: 0.07 us -> 0.63 us  [the longest x1 0.56 us: finish(): theirs = lax.ppermute(edges, 'rep', swap)]
    add x1 -> x0, other arithmetic: 0.51 us -> none  [per_device(): return (distances, sums + lax.ppermute(sums, 'rep', swap))]
    pallas_call x1, Pallas kernels: 2.48 us -> 2.1 us  [per_device(): pl.pallas_call(functools.partial(first_kernel, sizes), out_shape=(shape((...]
  transfers between devices with their start and end apart: 2 -> 2, of which waited for: 2 -> 1; matrix products, arithmetic and copies ran while one was open for 2% -> 0% of each run, Pallas kernels for 0% -> 0%
where the time goes in v5:
time: 31 us; the launch traced here: 30.7 us
  blocking collectives  24.3 us (78%)
  Pallas kernels  3.32 us (11%)
  between operations  1.31 us (4%)
  waiting for transfers between devices  1.2 us (4%)
  starting transfers between devices  0.63 us (2%)
    all_to_all x1, blocking collectives, finish(): lax.all_to_all(part.reshape(n_row * n_col, *part.shape[2:]), ('row', 'col...  16 us
    all_to_all x1, blocking collectives, per_device(): fresh = lax.all_to_all(part, 'col', 0, 0)  8.31 us
    pallas_call x1, Pallas kernels, per_device(): pl.pallas_call(functools.partial(first_kernel, sizes), out_shape=(shape((...  2.1 us
    ppermute x1, waiting for transfers between devices, per_device(): theirs = lax.ppermute(mine, 'rep', swap)  1.19 us
    pallas_call x1, Pallas kernels, per_device(): pl.pallas_call(final_kernel, out_shape=(shape((height, size), F32), shape...  0.65 us
  transfers between devices with their start and end apart: 2, of which 1 were waited for; matrix products, arithmetic and copies ran while one was open for 0% of the time, Pallas kernels for 0%

profile of v5, /device:TPU:0, one launch (start us, length us, event | category | flops | bytes accessed | tf_op | source)
XLA Modules:
  0.0 30.7 jit_solution(2448427655978909674)
XLA Ops:
  1.3 2.1 %round_one.1 = (bf16[33,128,128]{2,1,0:T(8,128)(2,1)S(1)}, bf16[8,64,128]{2,1,0:T(8,128)(2,1)S(1)}, bf16[64,128]{1,0:T(8,128)(2,1)S(1)}, bf16[4,4,32,128]{3,2,1,0:T(8,128)(2,1)S(1)}, s32[1]{0:T(128)S(4)}) custom-call(s32[1,64]{1,0:T(1,128)} %bitcast.10, s32[32,128,128]{2,1,0:T(8,128)} %weights.1, s32[32]{0:T(128)} %src.1, s32[32]{0:T(128)} %dst.1, ...), custom_call_target="tpu_custom_call" | custom-call | tf_op jit(solution)/shard_map/round_one/pallas_call | solution.py:169
  3.4 17.1 %conditional.1 = ((bf16[4,2,64,128]{3,2,1,0:T(8,128)(2,1)S(1)}, bf16[64,128]{1,0:T(8,128)(2,1)S(1)})) conditional(s32[]{:T(128)} %bitcast.5, (bf16[4,4,32,128]{3,2,1,0:T(8,128)(2,1)S(1)}, bf16[33,128,128]{2,1,0:T(8,128)(2,1)S(1)}, bf16[8,64,128]{2,1,0:T(8,128)(2,1)S(1)}, bf16[64,128]{1,0:T(8,128)(2,1)S(1)}) %tuple.13, ...), branch_computations={%region_0.0_spmd, %region_1.0_spmd} | conditional | bytes 4849712 | solution.py:224
  3.4 0.6 %collective-permute-start = (bf16[33,128,128]{2,1,0:T(8,128)(2,1)S(1)}, bf16[33,128,128]{2,1,0:T(8,128)(2,1)S(1)}, u32[]{:S(2)}, u32[]{:S(2)}) collective-permute-start(bf16[33,128,128]{2,1,0:T(8,128)(2,1)S(1)} %get-tuple-element.17.edges), channel_id=1, source_target_pairs={{0,1},{1,0},{2,3},{3,2},{4,5},{5,4},{6,7},{7,6},{8,9},{9,8},{10,11... | collective-permute-start | bytes 3244040 | tf_op jit(solution)/shard_map/cond/branch_0_fun/ppermute | solution.py:195
  4.0 16.0 %all_to_all.13 = bf16[16,32,128]{2,1,0:T(8,128)(2,1)S(1)} all-to-all(bf16[16,32,128]{2,1,0:T(8,128)(2,1)S(1)} %bitcast.9), channel_id=1, replica_groups=mesh['row'=4,'col'=4,'rep'=2] {'row','col'}, dimensions={0} | all-to-all | bytes 262144 | tf_op jit(solution)/shard_map/cond/branch_0_fun/all_to_all | solution.py:196
  19.9 0.0 collective-permute-done.theirs
  19.9 0.5 %round_two.1 = (bf16[4,2,64,128]{3,2,1,0:T(8,128)(2,1)S(1)}, bf16[64,128]{1,0:T(8,128)(2,1)S(1)}) custom-call(bf16[4,4,32,128]{3,2,1,0:T(8,128)(2,1)S(1)} %bitcast.8, bf16[8,64,128]{2,1,0:T(8,128)(2,1)S(1)} %get-tuple-element.15.hot, bf16[64,128]{1,0:T(8,128)(2,1)S(1)} %get-tuple-element.16.pick, bf16[33,128,128]{2,1,0:T(8,128)(2,1)S(1)} %get-tuple-element.17.edges, ...), custom_call_target="tpu_custom_call" | custom-call | tf_op jit(solution)/shard_map/cond/branch_0_fun/round_two/pallas_call | solution.py:199
  20.5 8.3 %all_to_all.15.fresh = bf16[4,2,64,128]{3,2,1,0:T(8,128)(2,1)S(1)} all-to-all(bf16[4,2,64,128]{3,2,1,0:T(8,128)(2,1)S(1)} %get-tuple-element.35), channel_id=1, replica_groups=mesh['row'=4,'col'=4,'rep'=2] {'col'}, dimensions={0} | all-to-all | bytes 262144 | tf_op jit(solution)/shard_map/all_to_all | solution.py:225
  28.8 0.1 collective-permute-start.2
  28.9 1.2 %collective-permute-done.2.theirs = bf16[2,64,128]{2,1,0:T(8,128)(2,1)S(1)} collective-permute-done((bf16[2,64,128]{2,1,0:T(8,128)(2,1)S(1)}, bf16[2,64,128]{2,1,0:T(8,128)(2,1)S(1)}, u32[]{:S(2)}, u32[]{:S(2)}) %collective-permute-start.2) | collective-permute-done | bytes 32800 | tf_op jit(solution)/shard_map/ppermute | solution.py:234
  30.1 0.7 %decode.1 = (f32[64,128]{1,0:T(8,128)}, f32[1,64]{1,0:T(1,128)}) custom-call(bf16[2,64,128]{2,1,0:T(8,128)(2,1)S(1)} %merge.1.mine, bf16[2,64,128]{2,1,0:T(8,128)(2,1)S(1)} %collective-permute-done.2.theirs), custom_call_target="tpu_custom_call" | custom-call | tf_op jit(solution)/shard_map/decode/pallas_call | solution.py:235
  (1 shorter events, 0.0 us)
Async XLA Ops:
  3.4 16.5 %collective-permute-start = (bf16[33,128,128]{2,1,0:T(8,128)(2,1)S(1)}, bf16[33,128,128]{2,1,0:T(8,128)(2,1)S(1)}, u32[]{:S(2)}, u32[]{:S(2)}) collective-permute-start(bf16[33,128,128]{2,1,0:T(8,128)(2,1)S(1)} %get-tuple-element.17.edges), channel_id=1, source_target_pairs={{0,1},{1,0},{2,3},{3,2},{4,5},{5,4},{6,7},{7,6},{8,9},{9,8},{10,11... | collective-permute-start | bytes 3244040 | tf_op jit(solution)/shard_map/cond/branch_0_fun/ppermute | solution.py:195
  28.8 1.3 %collective-permute-start.2 = (bf16[2,64,128]{2,1,0:T(8,128)(2,1)S(1)}, bf16[2,64,128]{2,1,0:T(8,128)(2,1)S(1)}, u32[]{:S(2)}, u32[]{:S(2)}) collective-permute-start(bf16[2,64,128]{2,1,0:T(8,128)(2,1)S(1)} %merge.1.mine), channel_id=1, source_target_pairs={{0,1},{1,0},{2,3},{3,2},{4,5},{5,4},{6,7},{7,6},{8,9},{9,8},{10,11... | collective-permute-start | bytes 98312 | tf_op jit(solution)/shard_map/ppermute | solution.py:234

commit v6 on v5

--- a/solution.py
+++ b/solution.py
@@ -156,7 +156,7 @@
     height = sources.shape[0]
     tiles, size, _ = tile_weights.shape
     slots = n_row * n_rep
-    room = min(height, max(16, 2 * height // n_col))
+    room = min(height, max(16, 3 * height // (2 * n_col)))
     assert n_rep == 2 and all(n & (n - 1) == 0 for n in (*sizes, size))
     vmem = pl.BlockSpec(memory_space=pltpu.VMEM)
     smem = pl.BlockSpec(memory_space=pltpu.SMEM)

time: 31 us -> 30.4 us (0.981)
  blocking collectives: 24.3 us -> 23.7 us
    all_to_all x1, blocking collectives: 16 us -> 15.4 us  [finish(): lax.all_to_all(part.reshape(n_row * n_col, *part.shape[2:]), ('row', 'col...]
where the time goes in v6:
time: 30.4 us; the launch traced here: 30.2 us
  blocking collectives  23.7 us (78%)
  Pallas kernels  3.32 us (11%)
  between operations  1.31 us (4%)
  waiting for transfers between devices  1.2 us (4%)
  starting transfers between devices  0.63 us (2%)
    all_to_all x1, blocking collectives, finish(): lax.all_to_all(part.reshape(n_row * n_col, *part.shape[2:]), ('row', 'col...  15.4 us
    all_to_all x1, blocking collectives, per_device(): fresh = lax.all_to_all(part, 'col', 0, 0)  8.31 us
    pallas_call x1, Pallas kernels, per_device(): pl.pallas_call(functools.partial(first_kernel, sizes), out_shape=(shape((...  2.1 us
    ppermute x1, waiting for transfers between devices, per_device(): theirs = lax.ppermute(mine, 'rep', swap)  1.19 us
    pallas_call x1, Pallas kernels, per_device(): pl.pallas_call(final_kernel, out_shape=(shape((height, size), F32), shape...  0.65 us
  transfers between devices with their start and end apart: 2, of which 1 were waited for; matrix products, arithmetic and copies ran while one was open for 0% of the time, Pallas kernels for 0%

profile of v6, /device:TPU:0, one launch (start us, length us, event | category | flops | bytes accessed | tf_op | source)
XLA Modules:
  0.0 30.2 jit_solution(17707141581706818253)
XLA Ops:
  1.3 2.1 %round_one.1 = (bf16[33,128,128]{2,1,0:T(8,128)(2,1)S(1)}, bf16[8,64,128]{2,1,0:T(8,128)(2,1)S(1)}, bf16[64,96]{1,0:T(8,128)(2,1)S(1)}, bf16[4,4,24,128]{3,2,1,0:T(8,128)(2,1)S(1)}, s32[1]{0:T(128)S(4)}) custom-call(s32[1,64]{1,0:T(1,128)} %bitcast.10, s32[32,128,128]{2,1,0:T(8,128)} %weights.1, s32[32]{0:T(128)} %src.1, s32[32]{0:T(128)} %dst.1, ...), custom_call_target="tpu_custom_call" | custom-call | tf_op jit(solution)/shard_map/round_one/pallas_call | solution.py:169
  3.4 16.5 %conditional.1 = ((bf16[4,2,64,128]{3,2,1,0:T(8,128)(2,1)S(1)}, bf16[64,128]{1,0:T(8,128)(2,1)S(1)})) conditional(s32[]{:T(128)} %bitcast.5, (bf16[4,4,24,128]{3,2,1,0:T(8,128)(2,1)S(1)}, bf16[33,128,128]{2,1,0:T(8,128)(2,1)S(1)}, bf16[8,64,128]{2,1,0:T(8,128)(2,1)S(1)}, bf16[64,96]{1,0:T(8,128)(2,1)S(1)}) %tuple.13, ...), branch_computations={%region_0.0_spmd, %region_1.0_spmd} | conditional | bytes 4849712 | solution.py:224
  3.4 0.6 %collective-permute-start = (bf16[33,128,128]{2,1,0:T(8,128)(2,1)S(1)}, bf16[33,128,128]{2,1,0:T(8,128)(2,1)S(1)}, u32[]{:S(2)}, u32[]{:S(2)}) collective-permute-start(bf16[33,128,128]{2,1,0:T(8,128)(2,1)S(1)} %get-tuple-element.17.edges), channel_id=1, source_target_pairs={{0,1},{1,0},{2,3},{3,2},{4,5},{5,4},{6,7},{7,6},{8,9},{9,8},{10,11... | collective-permute-start | bytes 3244040 | tf_op jit(solution)/shard_map/cond/branch_0_fun/ppermute | solution.py:195
  4.0 15.4 %all_to_all.13 = bf16[16,24,128]{2,1,0:T(8,128)(2,1)S(1)} all-to-all(bf16[16,24,128]{2,1,0:T(8,128)(2,1)S(1)} %bitcast.9), channel_id=1, replica_groups=mesh['row'=4,'col'=4,'rep'=2] {'row','col'}, dimensions={0} | all-to-all | bytes 196608 | tf_op jit(solution)/shard_map/cond/branch_0_fun/all_to_all | solution.py:196
  19.4 0.0 collective-permute-done.theirs
  19.4 0.5 %round_two.1 = (bf16[4,2,64,128]{3,2,1,0:T(8,128)(2,1)S(1)}, bf16[64,128]{1,0:T(8,128)(2,1)S(1)}) custom-call(bf16[4,4,24,128]{3,2,1,0:T(8,128)(2,1)S(1)} %bitcast.8, bf16[8,64,128]{2,1,0:T(8,128)(2,1)S(1)} %get-tuple-element.15.hot, bf16[64,96]{1,0:T(8,128)(2,1)S(1)} %get-tuple-element.16.pick, bf16[33,128,128]{2,1,0:T(8,128)(2,1)S(1)} %get-tuple-element.17.edges, ...), custom_call_target="tpu_custom_call" | custom-call | tf_op jit(solution)/shard_map/cond/branch_0_fun/round_two/pallas_call | solution.py:199
  19.9 8.3 %all_to_all.15.fresh = bf16[4,2,64,128]{3,2,1,0:T(8,128)(2,1)S(1)} all-to-all(bf16[4,2,64,128]{3,2,1,0:T(8,128)(2,1)S(1)} %get-tuple-element.35), channel_id=1, replica_groups=mesh['row'=4,'col'=4,'rep'=2] {'col'}, dimensions={0} | all-to-all | bytes 262144 | tf_op jit(solution)/shard_map/all_to_all | solution.py:225
  28.3 0.1 collective-permute-start.2
  28.3 1.2 %collective-permute-done.2.theirs = bf16[2,64,128]{2,1,0:T(8,128)(2,1)S(1)} collective-permute-done((bf16[2,64,128]{2,1,0:T(8,128)(2,1)S(1)}, bf16[2,64,128]{2,1,0:T(8,128)(2,1)S(1)}, u32[]{:S(2)}, u32[]{:S(2)}) %collective-permute-start.2) | collective-permute-done | bytes 32800 | tf_op jit(solution)/shard_map/ppermute | solution.py:234
  29.5 0.7 %decode.1 = (f32[64,128]{1,0:T(8,128)}, f32[1,64]{1,0:T(1,128)}) custom-call(bf16[2,64,128]{2,1,0:T(8,128)(2,1)S(1)} %merge.1.mine, bf16[2,64,128]{2,1,0:T(8,128)(2,1)S(1)} %collective-permute-done.2.theirs), custom_call_target="tpu_custom_call" | custom-call | tf_op jit(solution)/shard_map/decode/pallas_call | solution.py:235
  (1 shorter events, 0.0 us)
Async XLA Ops:
  3.4 16.0 %collective-permute-start = (bf16[33,128,128]{2,1,0:T(8,128)(2,1)S(1)}, bf16[33,128,128]{2,1,0:T(8,128)(2,1)S(1)}, u32[]{:S(2)}, u32[]{:S(2)}) collective-permute-start(bf16[33,128,128]{2,1,0:T(8,128)(2,1)S(1)} %get-tuple-element.17.edges), channel_id=1, source_target_pairs={{0,1},{1,0},{2,3},{3,2},{4,5},{5,4},{6,7},{7,6},{8,9},{9,8},{10,11... | collective-permute-start | bytes 3244040 | tf_op jit(solution)/shard_map/cond/branch_0_fun/ppermute | solution.py:195
  28.3 1.3 %collective-permute-start.2 = (bf16[2,64,128]{2,1,0:T(8,128)(2,1)S(1)}, bf16[2,64,128]{2,1,0:T(8,128)(2,1)S(1)}, u32[]{:S(2)}, u32[]{:S(2)}) collective-permute-start(bf16[2,64,128]{2,1,0:T(8,128)(2,1)S(1)} %merge.1.mine), channel_id=1, source_target_pairs={{0,1},{1,0},{2,3},{3,2},{4,5},{5,4},{6,7},{7,6},{8,9},{9,8},{10,11... | collective-permute-start | bytes 98312 | tf_op jit(solution)/shard_map/ppermute | solution.py:234

commit v7 on v6

--- a/solution.py
+++ b/solution.py
@@ -58,8 +58,9 @@
         )
         for c in range(CHUNKS)
     ]
-    for copy in copies:
-        copy.start()
+    live = count[0]
+    for c, copy in enumerate(copies):
+        pl.when(c * step < live)(copy.start)
     edges[...] = jnp.zeros_like(edges)
     for copy in firsts:
         copy.wait()
@@ -86,16 +87,19 @@
         at = lane + ((q % n_row * n_col + me) * n_rep + (rep ^ (q // n_row))) * size
         hot[q] = jnp.where(down == at, 2.0**TOP, 0.0).astype(BF16)
         few[q] = jnp.where(vertex == at[:room].astype(F32), 2.0**TOP, 0.0).astype(BF16)
-    live = count[0]
     for c, copy in enumerate(copies):
-        copy.wait()
-        for k in range(c * step, (c + 1) * step):
-            q = ((s_src[k] & 1) ^ rep) * n_row + lax.shift_right_logical(s_src[k], log(n_col * n_rep))
-            d = lax.shift_right_logical(s_dst[k], log(n_rep)) & (n_col - 1)
-            at = jnp.where(k < live, q * n_col + d, n_row * n_rep * n_col)
-            w = raw[k].astype(F32).astype(BF16)
-            coded = jnp.where(w > 0, jnp.exp2(BF16(-STEP) * w), BF16(0.0))
-            edges[at] = jnp.maximum(edges[at], coded)
+
+        @pl.when(c * step < live)
+        def _(c=c, copy=copy):
+            copy.wait()
+            for k in range(c * step, (c + 1) * step):
+                q = ((s_src[k] & 1) ^ rep) * n_row + lax.shift_right_logical(s_src[k], log(n_col * n_rep))
+                d = lax.shift_right_logical(s_dst[k], log(n_rep)) & (n_col - 1)
+                at = jnp.where(k < live, q * n_col + d, n_row * n_rep * n_col)
+                w = raw[k].astype(F32).astype(BF16)
+                coded = jnp.where(w > 0, jnp.exp2(BF16(-STEP) * w), BF16(0.0))
+                edges[at] = jnp.maximum(edges[at], coded)
+
     relax([few[q] for q in range(n_row * n_rep)], edges, best)
     spread(part, best)
 

time: 30.4 us -> 30.1 us (level)
  Pallas kernels: 3.32 us -> 2.86 us
    pallas_call x1, Pallas kernels: 2.1 us -> 1.64 us  [per_device(): pl.pallas_call(functools.partial(first_kernel, sizes), out_shape=(shape((...]
where the time goes in v7:
time: 30.1 us; the launch traced here: 29.7 us
  blocking collectives  23.7 us (79%)
  Pallas kernels  2.86 us (10%)
  between operations  1.31 us (4%)
  waiting for transfers between devices  1.2 us (4%)
  starting transfers between devices  0.63 us (2%)
    all_to_all x1, blocking collectives, finish(): lax.all_to_all(part.reshape(n_row * n_col, *part.shape[2:]), ('row', 'col...  15.4 us
    all_to_all x1, blocking collectives, per_device(): fresh = lax.all_to_all(part, 'col', 0, 0)  8.31 us
    pallas_call x1, Pallas kernels, per_device(): pl.pallas_call(functools.partial(first_kernel, sizes), out_shape=(shape((...  1.64 us
    ppermute x1, waiting for transfers between devices, per_device(): theirs = lax.ppermute(mine, 'rep', swap)  1.19 us
    pallas_call x1, Pallas kernels, per_device(): pl.pallas_call(final_kernel, out_shape=(shape((height, size), F32), shape...  0.65 us
  transfers between devices with their start and end apart: 2, of which 1 were waited for; matrix products, arithmetic and copies ran while one was open for 0% of the time, Pallas kernels for 0%

profile of v7, /device:TPU:0, one launch (start us, length us, event | category | flops | bytes accessed | tf_op | source)
XLA Modules:
  0.0 29.7 jit_solution(12430457796208323551)
XLA Ops:
  1.3 1.6 %round_one.1 = (bf16[33,128,128]{2,1,0:T(8,128)(2,1)S(1)}, bf16[8,64,128]{2,1,0:T(8,128)(2,1)S(1)}, bf16[64,96]{1,0:T(8,128)(2,1)S(1)}, bf16[4,4,24,128]{3,2,1,0:T(8,128)(2,1)S(1)}, s32[1]{0:T(128)S(4)}) custom-call(s32[1,64]{1,0:T(1,128)} %bitcast.10, s32[32,128,128]{2,1,0:T(8,128)} %weights.1, s32[32]{0:T(128)} %src.1, s32[32]{0:T(128)} %dst.1, ...), custom_call_target="tpu_custom_call" | custom-call | tf_op jit(solution)/shard_map/round_one/pallas_call | solution.py:173
  2.9 16.5 %conditional.1 = ((bf16[4,2,64,128]{3,2,1,0:T(8,128)(2,1)S(1)}, bf16[64,128]{1,0:T(8,128)(2,1)S(1)})) conditional(s32[]{:T(128)} %bitcast.5, (bf16[4,4,24,128]{3,2,1,0:T(8,128)(2,1)S(1)}, bf16[33,128,128]{2,1,0:T(8,128)(2,1)S(1)}, bf16[8,64,128]{2,1,0:T(8,128)(2,1)S(1)}, bf16[64,96]{1,0:T(8,128)(2,1)S(1)}) %tuple.13, ...), branch_computations={%region_0.0_spmd, %region_1.0_spmd} | conditional | bytes 4849712 | solution.py:228
  2.9 0.6 %collective-permute-start = (bf16[33,128,128]{2,1,0:T(8,128)(2,1)S(1)}, bf16[33,128,128]{2,1,0:T(8,128)(2,1)S(1)}, u32[]{:S(2)}, u32[]{:S(2)}) collective-permute-start(bf16[33,128,128]{2,1,0:T(8,128)(2,1)S(1)} %get-tuple-element.17.edges), channel_id=1, source_target_pairs={{0,1},{1,0},{2,3},{3,2},{4,5},{5,4},{6,7},{7,6},{8,9},{9,8},{10,11... | collective-permute-start | bytes 3244040 | tf_op jit(solution)/shard_map/cond/branch_0_fun/ppermute | solution.py:199
  3.5 15.4 %all_to_all.13 = bf16[16,24,128]{2,1,0:T(8,128)(2,1)S(1)} all-to-all(bf16[16,24,128]{2,1,0:T(8,128)(2,1)S(1)} %bitcast.9), channel_id=1, replica_groups=mesh['row'=4,'col'=4,'rep'=2] {'row','col'}, dimensions={0} | all-to-all | bytes 196608 | tf_op jit(solution)/shard_map/cond/branch_0_fun/all_to_all | solution.py:200
  18.9 0.0 collective-permute-done.theirs
  18.9 0.5 %round_two.1 = (bf16[4,2,64,128]{3,2,1,0:T(8,128)(2,1)S(1)}, bf16[64,128]{1,0:T(8,128)(2,1)S(1)}) custom-call(bf16[4,4,24,128]{3,2,1,0:T(8,128)(2,1)S(1)} %bitcast.8, bf16[8,64,128]{2,1,0:T(8,128)(2,1)S(1)} %get-tuple-element.15.hot, bf16[64,96]{1,0:T(8,128)(2,1)S(1)} %get-tuple-element.16.pick, bf16[33,128,128]{2,1,0:T(8,128)(2,1)S(1)} %get-tuple-element.17.edges, ...), custom_call_target="tpu_custom_call" | custom-call | tf_op jit(solution)/shard_map/cond/branch_0_fun/round_two/pallas_call | solution.py:203
  19.5 8.3 %all_to_all.15.fresh = bf16[4,2,64,128]{3,2,1,0:T(8,128)(2,1)S(1)} all-to-all(bf16[4,2,64,128]{3,2,1,0:T(8,128)(2,1)S(1)} %get-tuple-element.35), channel_id=1, replica_groups=mesh['row'=4,'col'=4,'rep'=2] {'col'}, dimensions={0} | all-to-all | bytes 262144 | tf_op jit(solution)/shard_map/all_to_all | solution.py:229
  27.8 0.1 collective-permute-start.2
  27.9 1.2 %collective-permute-done.2.theirs = bf16[2,64,128]{2,1,0:T(8,128)(2,1)S(1)} collective-permute-done((bf16[2,64,128]{2,1,0:T(8,128)(2,1)S(1)}, bf16[2,64,128]{2,1,0:T(8,128)(2,1)S(1)}, u32[]{:S(2)}, u32[]{:S(2)}) %collective-permute-start.2) | collective-permute-done | bytes 32800 | tf_op jit(solution)/shard_map/ppermute | solution.py:238
  29.1 0.7 %decode.1 = (f32[64,128]{1,0:T(8,128)}, f32[1,64]{1,0:T(1,128)}) custom-call(bf16[2,64,128]{2,1,0:T(8,128)(2,1)S(1)} %merge.1.mine, bf16[2,64,128]{2,1,0:T(8,128)(2,1)S(1)} %collective-permute-done.2.theirs), custom_call_target="tpu_custom_call" | custom-call | tf_op jit(solution)/shard_map/decode/pallas_call | solution.py:239
  (1 shorter events, 0.0 us)
Async XLA Ops:
  2.9 16.0 %collective-permute-start = (bf16[33,128,128]{2,1,0:T(8,128)(2,1)S(1)}, bf16[33,128,128]{2,1,0:T(8,128)(2,1)S(1)}, u32[]{:S(2)}, u32[]{:S(2)}) collective-permute-start(bf16[33,128,128]{2,1,0:T(8,128)(2,1)S(1)} %get-tuple-element.17.edges), channel_id=1, source_target_pairs={{0,1},{1,0},{2,3},{3,2},{4,5},{5,4},{6,7},{7,6},{8,9},{9,8},{10,11... | collective-permute-start | bytes 3244040 | tf_op jit(solution)/shard_map/cond/branch_0_fun/ppermute | solution.py:199
  27.8 1.3 %collective-permute-start.2 = (bf16[2,64,128]{2,1,0:T(8,128)(2,1)S(1)}, bf16[2,64,128]{2,1,0:T(8,128)(2,1)S(1)}, u32[]{:S(2)}, u32[]{:S(2)}) collective-permute-start(bf16[2,64,128]{2,1,0:T(8,128)(2,1)S(1)} %merge.1.mine), channel_id=1, source_target_pairs={{0,1},{1,0},{2,3},{3,2},{4,5},{5,4},{6,7},{7,6},{8,9},{9,8},{10,11... | collective-permute-start | bytes 98312 | tf_op jit(solution)/shard_map/ppermute | solution.py:238
